TPU v7x, 128 devices: a whole 4x4x4 slice. The times are simulated.
128 devices in a mesh: dp: 4 (over z), row: 8 (over x_lo, y), col: 4 (over x_hi, core).
Axes of the slice: x: 4 (x_hi: 2, x_lo: 2; x = x_hi * 2 + x_lo), y: 4, z: 4, core: 2. Of those that a mesh axis runs over, the one named last changes fastest.
Arguments:
- tokens: bfloat16 [32768, 6144], P(('dp', 'row', 'col')), may hold values from -60 to 60
- grads: bfloat16 [32768, 24576], P(('dp', 'row', 'col')), may hold values from -2 to 2
- weight_grad: bfloat16 [6144, 24576], P('row', ('dp', 'col')), may hold values from -0.5 to 0.5
Outputs:
- update: bfloat16 [6144, 24576], P('row', ('dp', 'col'))
All inputs are finite; a program needn't handle non-finite values.
Results may differ from a plain program's by a relative error of at most 0.00065.
The roundings to bfloat16 on the way count: a program that leaves them out, or rounds other values in their place, can miss the bound.
Values may be sent and summed in bfloat16 or wider, within the bound.
No kernel may reach another device: no remote copies, remote signals or barrier semaphores. Data moves between devices by JAX's collectives and lax.ppermute only.
A program may use at most 192 MiB of HBM per device.

v0:
```python
import functools
import math

import jax
import jax.numpy as jnp
from jax import lax
from jax.experimental import pallas as pl
from jax.experimental.pallas import tpu as pltpu
from jax.sharding import Mesh
from jax.sharding import PartitionSpec as P


D = 6144
F = 24576
TOKENS = 32768
BLOCK = 192
STEPS = 3
ALL = ("dp", "row_0", "row_1", "col_0", "col_1")
ROW = ("row_0", "row_1")
DP_COL = ("dp", "col_0", "col_1")

epsilon = 1e-06
damping = 0.01
trust_radius = 0.05


X_BITS = (0, 16, 2, 18)
Y_BITS = (0, 4, 8, 12)
Z_BITS = (0, 32, 64, 96)
HALF = BLOCK // 3
LANES = 128
IN_ROWS = BLOCK + 8
MIB = 1024 * 1024


def swap(array, near, far):
    return lax.ppermute(array, ALL, [(i, i ^ (far if i % 2 else near)) for i in range(128)])


def first(array, bits):
    return swap(array, bits[1], bits[3])


def second(array, bits):
    return swap(array, bits[3], bits[1])


def packed_pair(own, got, at):
    even = jnp.zeros((BLOCK, 256), jnp.float32)
    odd = jnp.zeros((BLOCK, 256), jnp.float32)
    for ref in (own, got):
        part = ref[:, at : at + 384]
        turned = part.T
        even += jnp.dot(turned[:BLOCK], part[:, :256], preferred_element_type=jnp.float32)
        odd += jnp.dot(turned[BLOCK:], part[:, 128:], preferred_element_type=jnp.float32)
    low = lax.broadcasted_iota(jnp.int32, (HALF, LANES), 1) < HALF
    e = [[even[HALF * i : HALF * (i + 1), LANES * j : LANES * (j + 1)] for j in range(2)] for i in range(3)]
    o = [[odd[HALF * i : HALF * (i + 1), LANES * j : LANES * (j + 1)] for j in range(2)] for i in range(3)]
    evens = (e[0][0], jnp.where(low, e[0][1], e[1][0]), jnp.where(low, e[2][1], e[2][0]))
    odds = (jnp.where(low, o[0][1], o[0][0]), jnp.where(low, o[1][1], o[0][1]), o[2][1])
    return evens, odds


def out_kernel(where, own, got, out):
    step = pl.program_id(0)
    for pair in range(2):
        pieces = packed_pair(own, got, pair * 384)
        for parity in range(2):
            at = 2 * pair + parity
            first = where[16 + step] + where[32 + at]
            second = where[24 + step] + where[36 + at]
            for i in range(3):
                out[first, second, HALF * i : HALF * (i + 1)] = pieces[parity][i]


def out_blocks(where, own, got):
    shape = (8, 4, BLOCK, LANES)
    return pl.pallas_call(
        out_kernel,
        grid_spec=pltpu.PrefetchScalarGridSpec(
            num_scalar_prefetch=1,
            grid=(8,),
            in_specs=[
                pl.BlockSpec((256, 768), lambda i, w: (0, w[i])),
                pl.BlockSpec((256, 768), lambda i, w: (0, w[8 + i])),
            ],
            out_specs=pl.BlockSpec(shape, lambda i, w: (0, 0, 0, 0)),
        ),
        out_shape=jax.ShapeDtypeStruct(shape, jnp.float32),
        cost_estimate=pl.CostEstimate(flops=10_000_000_000, bytes_accessed=10_000_000, transcendentals=0),
        compiler_params=pltpu.CompilerParams(vmem_limit_bytes=56 * MIB),
        name="cov_out",
    )(where, own, got)


def in_kernel(where, own, got, trace_own, trace_got, send, keep):
    y_slot = pl.program_id(0)
    u_y, v_y = y_slot // 2, lax.rem(y_slot, 2)
    trace = trace_own[...] + trace_got[...]
    for pair in range(2):
        pieces = packed_pair(own, got, pair * 384)
        for parity in range(2):
            piece = pieces[parity]
            slot = where[8 + 2 * pair + parity]

            def store(ref):
                for i in range(3):
                    ref[v_y, slot, HALF * i : HALF * (i + 1)] = piece[i]
                ref[v_y, slot, BLOCK:] = trace

            pl.when(u_y == 1)(functools.partial(store, send))
            pl.when(u_y == 0)(functools.partial(store, keep))


def in_blocks(where, own, got, trace_own, trace_got):
    shape = (2, 4, IN_ROWS, LANES)
    return pl.pallas_call(
        in_kernel,
        grid_spec=pltpu.PrefetchScalarGridSpec(
            num_scalar_prefetch=1,
            grid=(4,),
            in_specs=[
                pl.BlockSpec((256, 768), lambda i, w: (0, w[i])),
                pl.BlockSpec((256, 768), lambda i, w: (0, w[4 + i])),
                pl.BlockSpec((8, LANES), lambda i, w: (0, 0)),
                pl.BlockSpec((8, LANES), lambda i, w: (0, 0)),
            ],
            out_specs=[pl.BlockSpec(shape, lambda i, w: (0, 0, 0, 0))] * 2,
        ),
        out_shape=[jax.ShapeDtypeStruct(shape, jnp.float32)] * 2,
        cost_estimate=pl.CostEstimate(flops=5_000_000_000, bytes_accessed=5_000_000, transcendentals=0),
        compiler_params=pltpu.CompilerParams(vmem_limit_bytes=56 * MIB),
        name="cov_in",
    )(where, own, got, trace_own, trace_got)


def products_of(ref):
    value = ref[...]
    return lax.dot_general(value, value, (((1,), (1,)), ((), ())), preferred_element_type=jnp.float32)


def diagonal_rows(products):
    i = lax.broadcasted_iota(jnp.int32, (256, 256), 0)
    j = lax.broadcasted_iota(jnp.int32, (256, 256), 1)
    folded = jnp.sum(jnp.where(i == j, products, 0.0).reshape(32, 8, 256), axis=0)
    folded = folded[:, :128] + folded[:, 128:]
    return folded[:4] + folded[4:]


def tokens_kernel(where, tokens, out, total, products):
    step = pl.program_id(0)

    @pl.when(step == 0)
    def _():
        out[...] = tokens[...]
        products[...] = products_of(tokens)

    @pl.when(step == 1)
    def _():
        total[:4] = diagonal_rows(products[...] + products_of(tokens))
        total[4:] = jnp.zeros((4, LANES), jnp.float32)


def tokens_share(where, tokens):
    return pl.pallas_call(
        tokens_kernel,
        grid_spec=pltpu.PrefetchScalarGridSpec(
            num_scalar_prefetch=1,
            grid=(2,),
            in_specs=[pl.BlockSpec((256, D // 2), lambda i, w: (0, w[i]))],
            out_specs=[
                pl.BlockSpec((256, D // 2), lambda i, w: (0, 0)),
                pl.BlockSpec((8, LANES), lambda i, w: (0, 0)),
            ],
            scratch_shapes=[pltpu.VMEM((256, 256), jnp.float32)],
        ),
        out_shape=[
            jax.ShapeDtypeStruct((256, D // 2), jnp.bfloat16),
            jax.ShapeDtypeStruct((8, LANES), jnp.float32),
        ],
        cost_estimate=pl.CostEstimate(flops=500_000_000, bytes_accessed=5_000_000, transcendentals=0),
        compiler_params=pltpu.CompilerParams(vmem_limit_bytes=56 * MIB),
        name="tokens_share",
    )(where, tokens)


def grads_kernel(where, grads, before, one, two, total, products):
    step = pl.program_id(0)

    @pl.when(step == 0)
    def _():
        products[...] = jnp.zeros_like(products)

    @pl.when(step < 4)
    def _():
        one[...] = grads[...]

    @pl.when((step >= 4) & (step < 8))
    def _():
        two[...] = grads[...]

    products[...] += products_of(grads)

    @pl.when(step == 15)
    def _():
        total[:4] = before[:4]
        total[4:] = diagonal_rows(products[...])


def grads_share(where, grads, before):
    return pl.pallas_call(
        grads_kernel,
        grid_spec=pltpu.PrefetchScalarGridSpec(
            num_scalar_prefetch=1,
            grid=(16,),
            in_specs=[
                pl.BlockSpec((256, 1536), lambda i, w: (0, w[i])),
                pl.BlockSpec((8, LANES), lambda i, w: (0, 0)),
            ],
            out_specs=[
                pl.BlockSpec((256, 1536), lambda i, w: (0, jnp.minimum(i, 3))),
                pl.BlockSpec((256, 1536), lambda i, w: (0, jnp.clip(i - 4, 0, 3))),
                pl.BlockSpec((8, LANES), lambda i, w: (0, 0)),
            ],
            scratch_shapes=[pltpu.VMEM((256, 256), jnp.float32)],
        ),
        out_shape=[jax.ShapeDtypeStruct((256, 6144), jnp.bfloat16)] * 2
        + [jax.ShapeDtypeStruct((8, LANES), jnp.float32)],
        cost_estimate=pl.CostEstimate(flops=2_000_000_000, bytes_accessed=20_000_000, transcendentals=0),
        compiler_params=pltpu.CompilerParams(vmem_limit_bytes=56 * MIB),
        name="grads_share",
    )(where, grads, before)


def newton(pieces, trace, swapped, inward):
    total_in = jnp.sum(trace[:4], axis=(0, 1), keepdims=True) * (1.0 / TOKENS)
    total_out = jnp.sum(trace[4:], axis=(0, 1), keepdims=True) * (1.0 / TOKENS)
    ratio = jnp.sqrt((total_in / D + epsilon) / (total_out / F + epsilon))
    damp_root = math.sqrt(damping)
    shift = ratio * damp_root if inward else damp_root / ratio
    c = [jnp.where(swapped, pltpu.roll(value, HALF, 1), value) for value in pieces]
    t = [jnp.concatenate([value, value], axis=0).T for value in c]
    low = lax.broadcasted_iota(jnp.int32, (HALF, LANES), 1) < HALF
    zero = jnp.zeros((HALF, LANES), jnp.float32)
    rows = [
        [c[0], jnp.where(low, c[1], zero)],
        [jnp.where(low, t[0][HALF:], c[1]), jnp.where(low, t[2][HALF:], zero)],
        [jnp.where(low, t[1][:HALF], c[2]), jnp.where(low, c[2], zero)],
        [zero, zero],
    ]
    blocks = jnp.concatenate([jnp.concatenate(pair, axis=1) for pair in rows], axis=0)
    i = lax.broadcasted_iota(jnp.int32, (256, 256), 0)
    j = lax.broadcasted_iota(jnp.int32, (256, 256), 1)
    identity = jnp.where((i == j) & (i < BLOCK), 1.0, 0.0).astype(jnp.float32)
    matrix = blocks * (1.0 / TOKENS) + shift * identity
    total = jnp.sum(matrix * matrix, axis=(0, 1), keepdims=True)
    iterate = identity / jnp.sqrt(total)
    for _ in range(STEPS):
        product = jnp.dot(matrix, iterate, precision=lax.Precision.HIGHEST, preferred_element_type=jnp.float32)
        iterate = jnp.dot(
            iterate, 2.0 * identity - product, precision=lax.Precision.HIGHEST, preferred_element_type=jnp.float32
        )
    return iterate[:BLOCK, :BLOCK].astype(jnp.bfloat16)


def inverse_in_kernel(flag, one, two, out, trace_out):
    both = one[...] + two[...]
    trace = both[BLOCK:]
    trace_out[...] = trace
    pieces = [both[HALF * i : HALF * (i + 1)] for i in range(3)]
    out[...] = newton(pieces, trace, flag[0] == 1, True)


def inverse_out_kernel(flag, trace, slots, out):
    both = (slots[0] + slots[1] + (slots[2] + slots[3])) + (slots[4] + slots[5] + (slots[6] + slots[7]))
    pieces = [both[HALF * i : HALF * (i + 1)] for i in range(3)]
    value = newton(pieces, trace[...], flag[0] == 1, False)
    for i in range(8):
        out[i] = value


def inverse(kernel, flag, args, shapes):
    vmem = pl.BlockSpec(memory_space=pltpu.VMEM)
    return pl.pallas_call(
        kernel,
        in_specs=[pl.BlockSpec(memory_space=pltpu.SMEM)] + [vmem] * len(args),
        out_specs=[vmem] * len(shapes),
        out_shape=[jax.ShapeDtypeStruct(*shape) for shape in shapes],
        cost_estimate=pl.CostEstimate(flops=5_000_000_000, bytes_accessed=200_000, transcendentals=0),
    )(flag, *args)


def left_kernel(place, slots, weight, left, sums):
    for q in range(4):
        rows = slice(q * BLOCK, (q + 1) * BLOCK)
        left[rows, :] = jnp.dot(
            slots[place[q]], weight[rows, :], preferred_element_type=jnp.float32
        ).astype(jnp.bfloat16)
    for pair in range(4):
        at = 384 * pair
        turned = left[:, at : at + 384].T
        even = jnp.dot(turned[:BLOCK], weight[:, at : at + 256], preferred_element_type=jnp.float32)
        odd = jnp.dot(turned[BLOCK:], weight[:, at + 128 : at + 384], preferred_element_type=jnp.float32)
        sums[2 * pair] = even[:, :BLOCK]
        sums[2 * pair + 1] = odd[:, HALF:]


def left_product(place, slots, weight):
    vmem = pl.BlockSpec(memory_space=pltpu.VMEM)
    return pl.pallas_call(
        left_kernel,
        in_specs=[pl.BlockSpec(memory_space=pltpu.SMEM), vmem, vmem],
        out_specs=[vmem, vmem],
        out_shape=[
            jax.ShapeDtypeStruct(weight.shape, jnp.bfloat16),
            jax.ShapeDtypeStruct((8, BLOCK, BLOCK), jnp.float32),
        ],
        cost_estimate=pl.CostEstimate(flops=8_000_000_000, bytes_accessed=5_000_000, transcendentals=0),
        name="left",
    )(place, slots, weight)


def align_kernel(inverses, sums, total):
    product = jnp.zeros((BLOCK, BLOCK), jnp.float32)
    for block in range(8):
        product += inverses[block].astype(jnp.float32) * sums[block]
    total[...] = jnp.broadcast_to(jnp.sum(product, axis=(0, 1), keepdims=True), (128, LANES))


def align(inverses, sums):
    vmem = pl.BlockSpec(memory_space=pltpu.VMEM)
    return pl.pallas_call(
        align_kernel,
        in_specs=[vmem, vmem],
        out_specs=vmem,
        out_shape=jax.ShapeDtypeStruct((128, LANES), jnp.float32),
        cost_estimate=pl.CostEstimate(flops=500_000_000, bytes_accessed=1_500_000, transcendentals=0),
        name="align",
    )(inverses, sums)


def natural_kernel(left, inverses, totals, out):
    alignment = jnp.sum(totals[:, :1], axis=(0, 1), keepdims=True)
    scale = jnp.sqrt(trust_radius * D * F / alignment)
    zero = jnp.zeros((BLOCK, BLOCK), jnp.bfloat16)
    for pair in range(4):
        both = jnp.concatenate(
            [
                jnp.concatenate([inverses[2 * pair], zero], axis=1),
                jnp.concatenate([zero, inverses[2 * pair + 1]], axis=1),
            ],
            axis=0,
        )
        columns = slice(384 * pair, 384 * (pair + 1))
        natural = jnp.dot(left[:, columns], both, preferred_element_type=jnp.float32)
        out[:, columns] = (natural * scale).astype(jnp.bfloat16)


def natural_product(left, inverses, totals):
    vmem = pl.BlockSpec(memory_space=pltpu.VMEM)
    return pl.pallas_call(
        natural_kernel,
        in_specs=[vmem] * 3,
        out_specs=vmem,
        out_shape=jax.ShapeDtypeStruct(left.shape, jnp.bfloat16),
        cost_estimate=pl.CostEstimate(flops=3_000_000_000, bytes_accessed=10_000_000, transcendentals=0),
        name="natural",
    )(left, inverses, totals)


def ints(*values):
    return jnp.stack([jnp.asarray(v, jnp.int32) for v in values])


def side(far, at):
    return at // 2 if far else at % 2


def cubes(second, with_z):
    groups = {}
    for i in range(128):
        z, x_low, y, x_high, core = i // 32, i // 16 % 2, i // 4 % 4, i // 2 % 2, i % 2
        far = core == (0 if second else 1)
        axes = (z, 2 * x_high + x_low, y)
        rest = tuple(at % 2 ^ at // 2 if far else at // 2 for at in axes)
        order = tuple(side(far, at) for at in axes)
        if not with_z:
            rest, order = (z,) + rest[1:], order[1:]
        groups.setdefault((core, rest), {})[order] = i
    return [[members[k] for k in sorted(members)] for members in groups.values()]


def trade(array, groups):
    return lax.all_to_all(array, ALL, split_axis=0, concat_axis=0, tiled=True, axis_index_groups=groups)


def on_device(tokens, grads, weight_grad):
    z = lax.axis_index("dp")
    x_low = lax.axis_index("row_0")
    y = lax.axis_index("row_1")
    x_high = lax.axis_index("col_0")
    core = lax.axis_index("col_1")
    x = 2 * x_high + x_low
    other = 1 - core

    def first_of(c):
        return 1 + 2 * c

    def side_first(c, at):
        return jnp.where(c == 1, at // 2, lax.rem(at, 2))

    def side_second(c, at):
        return jnp.where(c == 0, at // 2, lax.rem(at, 2))

    def sides(c, at, to):
        mask = at ^ to
        moved = (mask == 2) | (mask == first_of(c))
        through = at ^ jnp.where(moved, first_of(c), 0)
        return side_first(c, through), side_second(c, to)

    def reached(c, at, last):
        places = []
        for through in (at, at ^ first_of(c)):
            there = side_second(c, through) == last
            places.append(jnp.where(there, through, through ^ (4 - first_of(c))))
        return places

    half, trace = tokens_share(ints(other, core), tokens)
    got_in = swap(half, 1, 1)
    chunks = [(at * 2 + h) * 2 for last in range(2) for at in reached(other, z, last) for h in range(2)]
    where = ints(*[at + other for at in chunks], *[at + core for at in chunks])
    one, two, trace = grads_share(where, grads, trace)
    got_trace = swap(trace, 1, 1)
    got_one = swap(one, 1, 1)
    got_two = swap(two, 1, 1)
    got_out = [got_one, got_two]

    x_sides = [sides(core, x, to) for to in range(4)]
    y_sides = [sides(core, y, to) for to in range(4)]

    def pair_of(u, at):
        one = at ^ (u * first_of(core))
        two = one ^ (4 - first_of(core))
        low = side_second(core, one) == 0
        return jnp.where(low, one, two), jnp.where(low, two, one)

    def relative(at, to):
        mask = at ^ to
        return ((mask == 2) | (mask == first_of(core))).astype(jnp.int32)

    y_order = [place for u in range(2) for place in pair_of(u, y)]
    where = ints(
        *[core * 4 + at for at in y_order], *y_order, *[2 * relative(x, at) + x_sides[at][1] for at in range(4)]
    )
    send, keep = in_blocks(where, tokens, got_in, trace, got_trace)
    y_side, x_side = side_second(core, y), side_second(core, x)

    def pick(array, at):
        return lax.dynamic_index_in_dim(array, at, 0, keepdims=False)

    got = first(send, Y_BITS)
    both = keep + got
    got = second(pick(both, 1 - y_side), Y_BITS)
    both = pick(both, y_side) + got
    got = first(both[2:], X_BITS)
    both = both[:2] + got
    got = second(pick(both, 1 - x_side), X_BITS)
    both = pick(both, x_side) + got
    got = first(both, Z_BITS)
    both = both + got
    got = second(both, Z_BITS)
    own, trace = inverse(
        inverse_in_kernel, ints(x_low), [both, got], [((BLOCK, BLOCK), jnp.bfloat16), ((8, LANES), jnp.float32)]
    )
    got = first(own, X_BITS)
    slots = jnp.stack([own, got])
    got = second(slots, X_BITS)
    slots = jnp.concatenate([slots, got], axis=0)
    got = swap(slots, 1, 1)
    slots = jnp.where(core == x_low, slots, got)
    g = first_of(x_low)
    order = (x, x ^ g, x ^ (4 - g), x ^ 2)
    place = ints(*[sum(jnp.where(order[s] == q, s, 0) for s in range(4)) for q in range(4)])
    left, sums = left_product(place, slots, weight_grad)

    parts = []
    for last in range(2):
        places = reached(core, z, last)
        where = ints(
            *[((at * 2 + to // 2) * 2 + core) * 2 + to % 2 for at in places for to in range(4)],
            *range(8),
            *[
                4 * side_first(core, through) + 2 * s[0]
                for through in (z, z ^ first_of(core))
                for s in x_sides
            ],
            *[2 * s[1] for _ in range(2) for s in x_sides],
            *[s[0] for s in y_sides],
            *[s[1] for s in y_sides],
        )
        blocks = out_blocks(where, grads, got_out[last])
        blocks = trade(blocks, cubes(False, True))
        parts.append(jnp.sum(blocks, axis=0))
    cube = jnp.concatenate(parts, axis=0)
    cube = trade(cube, cubes(True, True))
    (own,) = inverse(inverse_out_kernel, ints(lax.rem(y, 2)), [trace, cube], [((8, BLOCK, BLOCK), jnp.bfloat16)])
    inverses = lax.all_to_all(own, ROW, split_axis=0, concat_axis=0, tiled=True)
    total = align(inverses, sums)
    totals = lax.all_to_all(total, ALL, split_axis=0, concat_axis=0, tiled=True)
    return natural_product(left, inverses, totals)


def solution(mesh):
    finer = Mesh(mesh.devices.reshape(mesh.shape["dp"], 2, 4, 2, 2), ALL)
    placed = (P(ALL, None), P(ALL, None), P(ROW, DP_COL))
    return jax.shard_map(on_device, mesh=finer, in_specs=placed, out_specs=P(ROW, DP_COL), check_vma=False)
```

profile of v0, /device:TPU:1, one launch (start us, length us, event | category | flops | bytes accessed | tf_op | source)
XLA Modules:
  0.0 214.6 jit_solution(9101814357860728472)
XLA Ops:
  0.6 4.6 %tokens_share.1 = (bf16[256,3072]{1,0:T(8,128)(2,1)}, f32[8,128]{1,0:T(8,128)}) custom-call(s32[2]{0:T(128)} %pad_add_fusion.1.where, bf16[256,6144]{1,0:T(8,128)(2,1)} %own.3), custom_call_target="tpu_custom_call" | custom-call | flops 500000000 | bytes 5000000 | tf_op jit(solution)/shard_map/tokens_share/pallas_call | solution.py:165
  5.8 16.8 %grads_share.1 = (bf16[256,6144]{1,0:T(8,128)(2,1)}, bf16[256,6144]{1,0:T(8,128)(2,1)}, f32[8,128]{1,0:T(8,128)}) custom-call(s32[16]{0:T(128)} %stack.301.where, bf16[256,24576]{1,0:T(8,128)(2,1)} %own.5, f32[8,128]{1,0:T(8,128)} %get-tuple-element.17.before), custom_call_target="tpu_custom_call" | custom-call | flops 2000000000 | bytes 20000000 | tf_op jit(solution)/shard_map/grads_share/pallas_call | solution.py:211
  25.2 4.3 %collective-permute-done.11.got = bf16[256,6144]{1,0:T(8,128)(2,1)S(1)} collective-permute-done((bf16[256,6144]{1,0:T(8,128)(2,1)}, bf16[256,6144]{1,0:T(8,128)(2,1)S(1)}, u32[]{:S(2)}, u32[]{:S(2)}) %collective-permute-start.11) | collective-permute-done | bytes 3145760 | tf_op jit(solution)/shard_map/ppermute | solution.py:37
  31.1 9.3 %cov_out.2 = f32[8,4,192,128]{3,2,1,0:T(8,128)} custom-call(s32[40]{0:T(128)} %stack.330.where, bf16[256,24576]{1,0:T(8,128)(2,1)} %own.5, bf16[256,6144]{1,0:T(8,128)(2,1)} %copy-done.8), custom_call_target="tpu_custom_call" | custom-call | flops 10000000000 | bytes 10000000 | tf_op jit(solution)/shard_map/cov_out/pallas_call | solution.py:78
  40.4 9.9 %all-to-all-start = ((f32[8,4,192,128]{3,2,1,0:T(8,128)}), f32[8,4,192,128]{3,2,1,0:T(8,128)S(1)}, u32[]{:S(2)}, u32[]{:S(2)}) async-start(f32[8,4,192,128]{3,2,1,0:T(8,128)} %cov_out.2), calls=%async_computation | async-start | bytes 6291456 | tf_op jit(solution)/shard_map/all_to_all | solution.py:394
  52.4 6.2 %cov_in.1 = (f32[2,4,200,128]{3,2,1,0:T(8,128)}, f32[2,4,200,128]{3,2,1,0:T(8,128)}) custom-call(s32[12]{0:T(128)} %stack.281.where, bf16[256,6144]{1,0:T(8,128)(2,1)} %own.3, bf16[256,3072]{1,0:T(8,128)(2,1)} %collective-permute-done.got, f32[8,128]{1,0:T(8,128)} %get-tuple-element.18.trace_own, f32[8,128]{1,0:T(8,128)} %copy-done.11), custom_call_target="tpu_custom_call" | custom-call | flops 5000000000 | bytes 5000000 | tf_op jit(solution)/shard_map/cov_in/pallas_call | solution.py:117
  61.2 9.2 %cov_out.3 = f32[8,4,192,128]{3,2,1,0:T(8,128)} custom-call(s32[40]{0:T(128)} %stack.339.where, bf16[256,24576]{1,0:T(8,128)(2,1)} %own.5, bf16[256,6144]{1,0:T(8,128)(2,1)} %collective-permute-done.12.got), custom_call_target="tpu_custom_call" | custom-call | flops 10000000000 | bytes 10000000 | tf_op jit(solution)/shard_map/cov_out/pallas_call | solution.py:78
  70.4 7.0 %all-to-all-done = f32[8,4,192,128]{3,2,1,0:T(8,128)S(1)} async-done(((f32[8,4,192,128]{3,2,1,0:T(8,128)}), f32[8,4,192,128]{3,2,1,0:T(8,128)S(1)}, u32[]{:S(2)}, u32[]{:S(2)}) %all-to-all-start) | async-done | bytes 3145760 | tf_op jit(solution)/shard_map/all_to_all | solution.py:394
  77.4 4.4 %all-to-all-start.1 = ((f32[8,4,192,128]{3,2,1,0:T(8,128)}), f32[8,4,192,128]{3,2,1,0:T(8,128)}, u32[]{:S(2)}, u32[]{:S(2)}) async-start(f32[8,4,192,128]{3,2,1,0:T(8,128)} %cov_out.3), calls=%async_computation.1 | async-start | bytes 6291456 | tf_op jit(solution)/shard_map/all_to_all | solution.py:394
  85.3 15.4 %collective-permute-done.3 = f32[4,200,128]{2,1,0:T(8,128)} collective-permute-done((f32[4,200,128]{2,1,0:T(8,128)S(1)}, f32[4,200,128]{2,1,0:T(8,128)}, u32[]{:S(2)}, u32[]{:S(2)}) %collective-permute-start.3) | collective-permute-done | bytes 409632 | tf_op jit(solution)/shard_map/ppermute | solution.py:37
  103.3 5.4 %collective-permute-done.4 = f32[2,200,128]{2,1,0:T(8,128)} collective-permute-done((f32[2,200,128]{2,1,0:T(8,128)}, f32[2,200,128]{2,1,0:T(8,128)}, u32[]{:S(2)}, u32[]{:S(2)}) %collective-permute-start.4) | collective-permute-done | bytes 204832 | tf_op jit(solution)/shard_map/ppermute | solution.py:37
  110.5 3.5 %collective-permute-done.5 = f32[200,128]{1,0:T(8,128)S(1)} collective-permute-done((f32[200,128]{1,0:T(8,128)S(1)}, f32[200,128]{1,0:T(8,128)S(1)}, u32[]{:S(2)}, u32[]{:S(2)}) %collective-permute-start.5) | collective-permute-done | bytes 102432 | tf_op jit(solution)/shard_map/ppermute | solution.py:37
  114.9 3.4 %collective-permute-start.6 = (f32[200,128]{1,0:T(8,128)S(1)}, f32[200,128]{1,0:T(8,128)S(1)}, u32[]{:S(2)}, u32[]{:S(2)}) collective-permute-start(f32[200,128]{1,0:T(8,128)S(1)} %bitcast_add_fusion.1), channel_id=1, source_target_pairs={{0,32},{1,97},{2,34},{3,99},{4,36},{5,101},{6,38},{7,103},{8,40},{... | collective-permute-start | bytes 307208 | tf_op jit(solution)/shard_map/ppermute | solution.py:37
  120.5 3.5 %collective-permute-done.7.two = f32[200,128]{1,0:T(8,128)S(1)} collective-permute-done((f32[200,128]{1,0:T(8,128)S(1)}, f32[200,128]{1,0:T(8,128)S(1)}, u32[]{:S(2)}, u32[]{:S(2)}) %collective-permute-start.7) | collective-permute-done | bytes 102432 | tf_op jit(solution)/shard_map/ppermute | solution.py:37
  124.6 5.1 %shard_map.37 = (bf16[192,192]{1,0:T(8,128)(2,1)}, f32[8,128]{1,0:T(8,128)}) custom-call(s32[1]{0:T(128)} %bitcast.4.flag, f32[200,128]{1,0:T(8,128)} %copy-done.7, f32[200,128]{1,0:T(8,128)} %copy-done.9), custom_call_target="tpu_custom_call" | custom-call | flops 5000000000 | bytes 200000 | tf_op jit(solution)/shard_map/pallas_call | solution.py:284
  131.3 3.3 %collective-permute-done.8 = bf16[192,192]{1,0:T(8,128)(2,1)S(1)} collective-permute-done((bf16[192,192]{1,0:T(8,128)(2,1)}, bf16[192,192]{1,0:T(8,128)(2,1)S(1)}, u32[]{:S(2)}, u32[]{:S(2)}) %collective-permute-start.8) | collective-permute-done | bytes 73760 | tf_op jit(solution)/shard_map/ppermute | solution.py:37
  139.5 5.6 %all-to-all-start.2 = ((f32[8,192,128]{2,1,0:T(8,128)}), f32[8,192,128]{2,1,0:T(8,128)S(1)}, u32[]{:S(2)}, u32[]{:S(2)}) async-start(f32[8,192,128]{2,1,0:T(8,128)} %pad_maximum_fusion), calls=%async_computation.2 | async-start | bytes 1572864 | tf_op jit(solution)/shard_map/all_to_all | solution.py:394
  146.2 14.2 %collective-permute-start.10 = (bf16[4,192,192]{2,1,0:T(8,128)(2,1)S(1)}, bf16[4,192,192]{2,1,0:T(8,128)(2,1)S(1)}, u32[]{:S(2)}, u32[]{:S(2)}) collective-permute-start(bf16[4,192,192]{2,1,0:T(8,128)(2,1)S(1)} %pad_maximum_fusion.1), channel_id=1, source_target_pairs={{0,1},{1,0},{2,3},{3,2},{4,5},{5,4},{6,7},{7,6},{8,9},{9,8},{10,11... | collective-permute-start | bytes 884744 | tf_op jit(solution)/shard_map/ppermute | solution.py:37
  164.4 5.5 %shard_map.38 = bf16[8,192,192]{2,1,0:T(8,128)(2,1)} custom-call(s32[1]{0:T(128)} %bitcast.41.flag, f32[8,128]{1,0:T(8,128)} %get-tuple-element.23.trace, f32[8,192,128]{2,1,0:T(8,128)} %copy-done.6), custom_call_target="tpu_custom_call" | custom-call | flops 5000000000 | bytes 200000 | tf_op jit(solution)/shard_map/pallas_call | solution.py:284
  169.9 4.2 %all-to-all-start.3 = ((bf16[8,192,192]{2,1,0:T(8,128)(2,1)}), bf16[8,192,192]{2,1,0:T(8,128)(2,1)S(1)}, u32[]{:S(2)}, u32[]{:S(2)}) async-start(bf16[8,192,192]{2,1,0:T(8,128)(2,1)} %shard_map.38), calls=%async_computation.3 | async-start | bytes 1572864 | tf_op jit(solution)/shard_map/all_to_all | solution.py:507
  174.1 4.5 %left.1 = (bf16[768,1536]{1,0:T(8,128)(2,1)}, f32[8,192,192]{2,1,0:T(8,128)}) custom-call(s32[4]{0:T(128)} %pad_add_fusion.place, bf16[4,192,192]{2,1,0:T(8,128)(2,1)} %broadcast_select_fusion.slots, bf16[768,1536]{1,0:T(8,128)(2,1)} %weight.1), custom_call_target="tpu_custom_call" | custom-call | flops 8000000000 | bytes 5000000 | tf_op jit(solution)/shard_map/left/pallas_call | solution.py:310
  178.6 3.8 %all-to-all-done.3.inverses = bf16[8,192,192]{2,1,0:T(8,128)(2,1)S(1)} async-done(((bf16[8,192,192]{2,1,0:T(8,128)(2,1)}), bf16[8,192,192]{2,1,0:T(8,128)(2,1)S(1)}, u32[]{:S(2)}, u32[]{:S(2)}) %all-to-all-start.3) | async-done | bytes 589856 | tf_op jit(solution)/shard_map/all_to_all | solution.py:507
  185.9 23.7 %all_to_all.31 = f32[128,1,128]{2,1,0:T(1,128)} all-to-all(f32[128,1,128]{2,1,0:T(1,128)} %bitcast.88), channel_id=1, replica_groups=mesh['dp'=4,'row_0'=2,'row_1'=4,'col_0'=2,'col_1'=2] {'dp','row_0','row_..., dimensions={0} | all-to-all | bytes 131072 | tf_op jit(solution)/shard_map/all_to_all | solution.py:509
  209.6 5.0 %natural.1 = bf16[768,1536]{1,0:T(8,128)(2,1)} custom-call(bf16[768,1536]{1,0:T(8,128)(2,1)} %get-tuple-element.22.left, bf16[8,192,192]{2,1,0:T(8,128)(2,1)} %copy-done.1, f32[128,128]{1,0:T(8,128)} %bitcast.89), custom_call_target="tpu_custom_call" | custom-call | flops 3000000000 | bytes 10000000 | tf_op jit(solution)/shard_map/natural/pallas_call | solution.py:361
  (65 shorter events, 36.4 us)
Async XLA Ops:
  22.6 6.9 %collective-permute-start.11 = (bf16[256,6144]{1,0:T(8,128)(2,1)}, bf16[256,6144]{1,0:T(8,128)(2,1)S(1)}, u32[]{:S(2)}, u32[]{:S(2)}) collective-permute-start(bf16[256,6144]{1,0:T(8,128)(2,1)} %get-tuple-element.24), channel_id=1, source_target_pairs={{0,1},{1,0},{2,3},{3,2},{4,5},{5,4},{6,7},{7,6},{8,9},{9,8},{10,11... | collective-permute-start | bytes 9437192 | tf_op jit(solution)/shard_map/ppermute | solution.py:37
  24.0 37.3 %collective-permute-start.12 = (bf16[256,6144]{1,0:T(8,128)(2,1)}, bf16[256,6144]{1,0:T(8,128)(2,1)}, u32[]{:S(2)}, u32[]{:S(2)}) collective-permute-start(bf16[256,6144]{1,0:T(8,128)(2,1)} %get-tuple-element.25), channel_id=1, source_target_pairs={{0,1},{1,0},{2,3},{3,2},{4,5},{5,4},{6,7},{7,6},{8,9},{9,8},{10,11... | collective-permute-start | bytes 9437192 | tf_op jit(solution)/shard_map/ppermute | solution.py:37
  24.0 27.8 %collective-permute-start = (bf16[256,3072]{1,0:T(8,128)(2,1)}, bf16[256,3072]{1,0:T(8,128)(2,1)}, u32[]{:S(2)}, u32[]{:S(2)}) collective-permute-start(bf16[256,3072]{1,0:T(8,128)(2,1)} %get-tuple-element.16), channel_id=1, source_target_pairs={{0,1},{1,0},{2,3},{3,2},{4,5},{5,4},{6,7},{7,6},{8,9},{9,8},{10,11... | collective-permute-start | bytes 4718600 | tf_op jit(solution)/shard_map/ppermute | solution.py:37
  29.5 1.7 copy-start.8
  40.4 9.9 %copy-start.10 = (f32[8,128]{1,0:T(8,128)S(1)}, f32[8,128]{1,0:T(8,128)}, u32[]{:S(2)}) copy-start(f32[8,128]{1,0:T(8,128)} %get-tuple-element.18.trace_own) | copy-start | bytes 12292
  40.4 37.0 %all-to-all-start = ((f32[8,4,192,128]{3,2,1,0:T(8,128)}), f32[8,4,192,128]{3,2,1,0:T(8,128)S(1)}, u32[]{:S(2)}, u32[]{:S(2)}) async-start(f32[8,4,192,128]{3,2,1,0:T(8,128)} %cov_out.2), calls=%async_computation | async-start | bytes 6291456 | tf_op jit(solution)/shard_map/all_to_all | solution.py:394
  50.3 1.4 collective-permute-start.1
  58.6 23.2 %collective-permute-start.2 = (f32[2,4,200,128]{3,2,1,0:T(8,128)}, f32[2,4,200,128]{3,2,1,0:T(8,128)}, u32[]{:S(2)}, u32[]{:S(2)}) collective-permute-start(f32[2,4,200,128]{3,2,1,0:T(8,128)} %get-tuple-element.20), channel_id=1, source_target_pairs={{0,4},{1,13},{2,6},{3,15},{4,0},{5,9},{6,2},{7,11},{8,12},{9,5},{1... | collective-permute-start | bytes 2457608 | tf_op jit(solution)/shard_map/ppermute | solution.py:37
  77.4 59.1 %all-to-all-start.1 = ((f32[8,4,192,128]{3,2,1,0:T(8,128)}), f32[8,4,192,128]{3,2,1,0:T(8,128)}, u32[]{:S(2)}, u32[]{:S(2)}) async-start(f32[8,4,192,128]{3,2,1,0:T(8,128)} %cov_out.3), calls=%async_computation.1 | async-start | bytes 6291456 | tf_op jit(solution)/shard_map/all_to_all | solution.py:394
  83.3 0.9 copy-start
  84.2 16.5 %collective-permute-start.3 = (f32[4,200,128]{2,1,0:T(8,128)S(1)}, f32[4,200,128]{2,1,0:T(8,128)}, u32[]{:S(2)}, u32[]{:S(2)}) collective-permute-start(f32[4,200,128]{2,1,0:T(8,128)S(1)} %dynamic-slice_bitcast_fusion), channel_id=1, source_target_pairs={{0,12},{1,5},{2,14},{3,7},{4,8},{5,1},{6,10},{7,3},{8,4},{9,13},{1... | collective-permute-start | bytes 1228808 | tf_op jit(solution)/shard_map/ppermute | solution.py:37
  102.6 6.1 %collective-permute-start.4 = (f32[2,200,128]{2,1,0:T(8,128)}, f32[2,200,128]{2,1,0:T(8,128)}, u32[]{:S(2)}, u32[]{:S(2)}) collective-permute-start(f32[2,200,128]{2,1,0:T(8,128)} %slice.9), channel_id=1, source_target_pairs={{0,16},{1,19},{2,18},{3,17},{4,20},{5,23},{6,22},{7,21},{8,24},{9,... | collective-permute-start | bytes 614408 | tf_op jit(solution)/shard_map/ppermute | solution.py:37
  110.4 3.6 %collective-permute-start.5 = (f32[200,128]{1,0:T(8,128)S(1)}, f32[200,128]{1,0:T(8,128)S(1)}, u32[]{:S(2)}, u32[]{:S(2)}) collective-permute-start(f32[200,128]{1,0:T(8,128)S(1)} %dynamic-slice_bitcast_fusion.1), channel_id=1, source_target_pairs={{0,18},{1,17},{2,16},{3,19},{4,22},{5,21},{6,20},{7,23},{8,26},{9,... | collective-permute-start | bytes 307208 | tf_op jit(solution)/shard_map/ppermute | solution.py:37
  114.9 5.5 %collective-permute-start.6 = (f32[200,128]{1,0:T(8,128)S(1)}, f32[200,128]{1,0:T(8,128)S(1)}, u32[]{:S(2)}, u32[]{:S(2)}) collective-permute-start(f32[200,128]{1,0:T(8,128)S(1)} %bitcast_add_fusion.1), channel_id=1, source_target_pairs={{0,32},{1,97},{2,34},{3,99},{4,36},{5,101},{6,38},{7,103},{8,40},{... | collective-permute-start | bytes 307208 | tf_op jit(solution)/shard_map/ppermute | solution.py:37
  120.3 3.6 %copy-start.7 = (f32[200,128]{1,0:T(8,128)}, f32[200,128]{1,0:T(8,128)S(1)}, u32[]{:S(2)}) copy-start(f32[200,128]{1,0:T(8,128)S(1)} %add.353.one) | copy-start | bytes 307204
  120.4 3.6 %collective-permute-start.7 = (f32[200,128]{1,0:T(8,128)S(1)}, f32[200,128]{1,0:T(8,128)S(1)}, u32[]{:S(2)}, u32[]{:S(2)}) collective-permute-start(f32[200,128]{1,0:T(8,128)S(1)} %add.353.one), channel_id=1, source_target_pairs={{0,96},{1,33},{2,98},{3,35},{4,100},{5,37},{6,102},{7,39},{8,104},... | collective-permute-start | bytes 307208 | tf_op jit(solution)/shard_map/ppermute | solution.py:37
  129.7 4.9 %collective-permute-start.8 = (bf16[192,192]{1,0:T(8,128)(2,1)}, bf16[192,192]{1,0:T(8,128)(2,1)S(1)}, u32[]{:S(2)}, u32[]{:S(2)}) collective-permute-start(bf16[192,192]{1,0:T(8,128)(2,1)} %get-tuple-element.21), channel_id=1, source_target_pairs={{0,16},{1,19},{2,18},{3,17},{4,20},{5,23},{6,22},{7,21},{8,24},{9,... | collective-permute-start | bytes 221192 | tf_op jit(solution)/shard_map/ppermute | solution.py:37
  134.6 1.6 copy-start.3
  136.2 8.9 %collective-permute-start.9 = (bf16[2,192,192]{2,1,0:T(8,128)(2,1)}, bf16[2,192,192]{2,1,0:T(8,128)(2,1)}, u32[]{:S(2)}, u32[]{:S(2)}) collective-permute-start(bf16[2,192,192]{2,1,0:T(8,128)(2,1)} %pad_maximum_fusion.2), channel_id=1, source_target_pairs={{0,18},{1,17},{2,16},{3,19},{4,22},{5,21},{6,20},{7,23},{8,26},{9,... | collective-permute-start | bytes 442376 | tf_op jit(solution)/shard_map/ppermute | solution.py:37
  136.4 8.7 %copy-start.2 = (bf16[192,192]{1,0:T(8,128)(2,1)S(1)}, bf16[192,192]{1,0:T(8,128)(2,1)}, u32[]{:S(2)}) copy-start(bf16[192,192]{1,0:T(8,128)(2,1)} %get-tuple-element.21) | copy-start | bytes 221188
  136.4 8.7 %copy-start.4 = (bf16[192,192]{1,0:T(8,128)(2,1)S(1)}, bf16[192,192]{1,0:T(8,128)(2,1)}, u32[]{:S(2)}) copy-start(bf16[192,192]{1,0:T(8,128)(2,1)} %copy-done.3) | copy-start | bytes 221188
  139.5 24.0 %all-to-all-start.2 = ((f32[8,192,128]{2,1,0:T(8,128)}), f32[8,192,128]{2,1,0:T(8,128)S(1)}, u32[]{:S(2)}, u32[]{:S(2)}) async-start(f32[8,192,128]{2,1,0:T(8,128)} %pad_maximum_fusion), calls=%async_computation.2 | async-start | bytes 1572864 | tf_op jit(solution)/shard_map/all_to_all | solution.py:394
  146.2 15.6 %collective-permute-start.10 = (bf16[4,192,192]{2,1,0:T(8,128)(2,1)S(1)}, bf16[4,192,192]{2,1,0:T(8,128)(2,1)S(1)}, u32[]{:S(2)}, u32[]{:S(2)}) collective-permute-start(bf16[4,192,192]{2,1,0:T(8,128)(2,1)S(1)} %pad_maximum_fusion.1), channel_id=1, source_target_pairs={{0,1},{1,0},{2,3},{3,2},{4,5},{5,4},{6,7},{7,6},{8,9},{9,8},{10,11... | collective-permute-start | bytes 884744 | tf_op jit(solution)/shard_map/ppermute | solution.py:37
  169.9 12.6 %all-to-all-start.3 = ((bf16[8,192,192]{2,1,0:T(8,128)(2,1)}), bf16[8,192,192]{2,1,0:T(8,128)(2,1)S(1)}, u32[]{:S(2)}, u32[]{:S(2)}) async-start(bf16[8,192,192]{2,1,0:T(8,128)(2,1)} %shard_map.38), calls=%async_computation.3 | async-start | bytes 1572864 | tf_op jit(solution)/shard_map/all_to_all | solution.py:507
  (5 other events, 3.7 us)
where the time goes:
time: 216 us; the launch traced here: 215 us
  Pallas kernels  68.8 us (32%)
  starting transfers between devices  49.9 us (23%)
  waiting for transfers between devices  49 us (23%)
  blocking collectives  23.7 us (11%)
  other arithmetic  13.3 us (6%)
  local copies, waits for them, and re-layouts  9.59 us (4%)
    ppermute x13, waiting for transfers between devices, swap(): lax.ppermute(array, ALL, [(i, i ^ (far if i % 2 else near)) for i in rang...  38.2 us
    ppermute x13, starting transfers between devices, swap(): lax.ppermute(array, ALL, [(i, i ^ (far if i % 2 else near)) for i in rang...  25.7 us
    all_to_all x1, blocking collectives, on_device(): totals = lax.all_to_all(total, ALL, split_axis=0, concat_axis=0, tiled=True)  23.7 us
    all_to_all x3, starting transfers between devices, trade(): lax.all_to_all(array, ALL, split_axis=0, concat_axis=0, tiled=True, axis_...  20 us
    pallas_call x2, Pallas kernels, out_blocks(): pl.pallas_call(out_kernel, grid_spec=pltpu.PrefetchScalarGridSpec(num_sca...  18.4 us
    pallas_call x1, Pallas kernels, grads_share(): pl.pallas_call(grads_kernel, grid_spec=pltpu.PrefetchScalarGridSpec(num_s...  16.8 us
    pallas_call x2, Pallas kernels, inverse(): pl.pallas_call(kernel, in_specs=[pl.BlockSpec(memory_space=pltpu.SMEM)] +...  10.7 us
    all_to_all x3, waiting for transfers between devices, trade(): lax.all_to_all(array, ALL, split_axis=0, concat_axis=0, tiled=True, axis_...  6.98 us
  transfers between devices with their start and end apart: 17, of which 10 were waited for; matrix products, arithmetic and copies ran while one was open for 7% of the time, Pallas kernels for 16%

commit v1 on v0

v1 whole, which is shorter than its diff:
```python
import functools
import math

import jax
import jax.numpy as jnp
import numpy as np
from jax import lax
from jax.experimental import pallas as pl
from jax.experimental.pallas import tpu as pltpu
from jax.sharding import Mesh
from jax.sharding import PartitionSpec as P


D = 6144
F = 24576
TOKENS = 32768
BLOCK = 192
STEPS = 3
ALL = ("dp", "row_0", "row_1", "col_0", "col_1")
ROW = ("row_0", "row_1")
DP_COL = ("dp", "col_0", "col_1")

epsilon = 1e-06
damping = 0.01
trust_radius = 0.05


X_BITS = (0, 16, 2, 18)
Y_BITS = (0, 4, 8, 12)
Z_BITS = (0, 32, 64, 96)
HALF = BLOCK // 3
LANES = 128
IN_ROWS = BLOCK + 8
MIB = 1024 * 1024
OUT_SCALE = 2.0 ** 13 / 512.0


def swap(array, near, far):
    return lax.ppermute(array, ALL, [(i, i ^ (far if i % 2 else near)) for i in range(128)])


def first(array, bits):
    return swap(array, bits[1], bits[3])


def second(array, bits):
    return swap(array, bits[3], bits[1])


def packed_pair(own, got, at):
    even = jnp.zeros((BLOCK, 256), jnp.float32)
    odd = jnp.zeros((BLOCK, 256), jnp.float32)
    for ref in (own, got):
        part = ref[:, at : at + 384]
        turned = part.T
        even += jnp.dot(turned[:BLOCK], part[:, :256], preferred_element_type=jnp.float32)
        odd += jnp.dot(turned[BLOCK:], part[:, 128:], preferred_element_type=jnp.float32)
    low = lax.broadcasted_iota(jnp.int32, (HALF, LANES), 1) < HALF
    e = [[even[HALF * i : HALF * (i + 1), LANES * j : LANES * (j + 1)] for j in range(2)] for i in range(3)]
    o = [[odd[HALF * i : HALF * (i + 1), LANES * j : LANES * (j + 1)] for j in range(2)] for i in range(3)]
    evens = (e[0][0], jnp.where(low, e[0][1], e[1][0]), jnp.where(low, e[2][1], e[2][0]))
    odds = (jnp.where(low, o[0][1], o[0][0]), jnp.where(low, o[1][1], o[0][1]), o[2][1])
    return evens, odds


def out_kernel(index, own, got, out):
    step = pl.program_id(0)
    for pair in range(2):
        pieces = packed_pair(own, got, pair * 384)
        for parity in range(2):
            at = 2 * pair + parity
            first = index[FIRST_AT + step] + index[Y_FIRST_AT + at]
            second = index[SECOND_AT + step] + index[Y_SECOND_AT + at]
            for i in range(3):
                out[first, second, HALF * i : HALF * (i + 1)] = pieces[parity][i]


def out_blocks(index, last, own, got):
    shape = (8, 4, BLOCK, LANES)
    base = OWN_AT + 8 * last
    return pl.pallas_call(
        out_kernel,
        grid_spec=pltpu.PrefetchScalarGridSpec(
            num_scalar_prefetch=1,
            grid=(8,),
            in_specs=[
                pl.BlockSpec((256, 768), lambda i, w: (0, w[base + i])),
                pl.BlockSpec((256, 768), lambda i, w: (0, i)),
            ],
            out_specs=pl.BlockSpec(shape, lambda i, w: (0, 0, 0, 0)),
        ),
        out_shape=jax.ShapeDtypeStruct(shape, jnp.float32),
        cost_estimate=pl.CostEstimate(flops=10_000_000_000, bytes_accessed=10_000_000, transcendentals=0),
        compiler_params=pltpu.CompilerParams(vmem_limit_bytes=56 * MIB),
        name="cov_out",
    )(index, own, got)


def in_kernel(index, own, got, trace_own, trace_got, send, keep):
    slot = index[Y_SLOT_AT + pl.program_id(0)]
    trace = trace_own[...] + trace_got[...]
    for pair in range(2):
        pieces = packed_pair(own, got, pair * 384)
        for parity in range(2):
            piece = pieces[parity]
            u_x = index[X_MOVED_AT + 2 * pair + parity]
            v_x = index[X_SECOND_AT + 2 * pair + parity]

            def store(ref):
                for i in range(3):
                    ref[v_x, slot, HALF * i : HALF * (i + 1)] = piece[i]
                ref[v_x, slot, BLOCK:] = trace

            pl.when(u_x == 1)(functools.partial(store, send))
            pl.when(u_x == 0)(functools.partial(store, keep))


def in_blocks(index, own, got, trace_own, trace_got):
    shape = (2, 4, IN_ROWS, LANES)
    return pl.pallas_call(
        in_kernel,
        grid_spec=pltpu.PrefetchScalarGridSpec(
            num_scalar_prefetch=1,
            grid=(4,),
            in_specs=[
                pl.BlockSpec((256, 768), lambda i, w: (0, w[IN_AT] + i)),
                pl.BlockSpec((256, 768), lambda i, w: (0, i)),
                pl.BlockSpec((8, LANES), lambda i, w: (0, 0)),
                pl.BlockSpec((8, LANES), lambda i, w: (0, 0)),
            ],
            out_specs=[pl.BlockSpec(shape, lambda i, w: (0, 0, 0, 0))] * 2,
        ),
        out_shape=[jax.ShapeDtypeStruct(shape, jnp.float32)] * 2,
        cost_estimate=pl.CostEstimate(flops=5_000_000_000, bytes_accessed=5_000_000, transcendentals=0),
        compiler_params=pltpu.CompilerParams(vmem_limit_bytes=16 * MIB),
        name="cov_in",
    )(index, own, got, trace_own, trace_got)


def squares_of(ref):
    sums = [jnp.zeros((16, LANES), jnp.float32) for _ in range(4)]
    count = 0
    for row in range(0, ref.shape[0], 16):
        for at in range(0, ref.shape[1], LANES):
            value = ref[row : row + 16, at : at + LANES].astype(jnp.float32)
            sums[count % 4] += value * value
            count += 1
    total = (sums[0] + sums[1]) + (sums[2] + sums[3])
    total = total[:8] + total[8:]
    return total[:4] + total[4:]


def tokens_kernel(index, tokens, out, total):
    @pl.when(pl.program_id(0) == 0)
    def _():
        total[...] = jnp.zeros_like(total)

    at = pl.multiple_of(index[TOKENS_AT] * (D // 2), D // 2)
    out[...] = tokens[:, pl.ds(at, D // 2)]
    total[:4] += squares_of(tokens)


def tokens_share(index, tokens):
    return pl.pallas_call(
        tokens_kernel,
        grid_spec=pltpu.PrefetchScalarGridSpec(
            num_scalar_prefetch=1,
            grid=(4,),
            in_specs=[pl.BlockSpec((64, D), lambda i, w: (i, 0))],
            out_specs=[
                pl.BlockSpec((64, D // 2), lambda i, w: (i, 0)),
                pl.BlockSpec((8, LANES), lambda i, w: (0, 0)),
            ],
        ),
        out_shape=[
            jax.ShapeDtypeStruct((256, D // 2), jnp.bfloat16),
            jax.ShapeDtypeStruct((8, LANES), jnp.float32),
        ],
        cost_estimate=pl.CostEstimate(flops=500_000_000, bytes_accessed=5_000_000, transcendentals=0),
        compiler_params=pltpu.CompilerParams(vmem_limit_bytes=60 * MIB),
        name="tokens_share",
    )(index, tokens)


def grads_kernel(index, grads, before, one, two, total):
    @pl.when(pl.program_id(0) == 0)
    def _():
        total[...] = before[...]

    for chunk in range(4):
        for half, out in enumerate((one, two)):
            at = pl.multiple_of(index[GRADS_AT + 4 * half + chunk] * 1536, 1536)
            out[:, 1536 * chunk : 1536 * (chunk + 1)] = grads[:, pl.ds(at, 1536)]
    total[4:] += squares_of(grads)


def grads_share(index, grads, before):
    rows = 32
    return pl.pallas_call(
        grads_kernel,
        grid_spec=pltpu.PrefetchScalarGridSpec(
            num_scalar_prefetch=1,
            grid=(256 // rows,),
            in_specs=[
                pl.BlockSpec((rows, F), lambda i, w: (i, 0)),
                pl.BlockSpec((8, LANES), lambda i, w: (0, 0)),
            ],
            out_specs=[
                pl.BlockSpec((rows, 6144), lambda i, w: (i, 0)),
                pl.BlockSpec((rows, 6144), lambda i, w: (i, 0)),
                pl.BlockSpec((8, LANES), lambda i, w: (0, 0)),
            ],
        ),
        out_shape=[jax.ShapeDtypeStruct((256, 6144), jnp.bfloat16)] * 2
        + [jax.ShapeDtypeStruct((8, LANES), jnp.float32)],
        cost_estimate=pl.CostEstimate(flops=2_000_000_000, bytes_accessed=20_000_000, transcendentals=0),
        compiler_params=pltpu.CompilerParams(vmem_limit_bytes=56 * MIB),
        name="grads_share",
    )(index, grads, before)


def newton(pieces, trace, swapped, inward):
    total_in = jnp.sum(trace[:4], axis=(0, 1), keepdims=True) * (1.0 / TOKENS)
    total_out = jnp.sum(trace[4:], axis=(0, 1), keepdims=True) * (1.0 / TOKENS)
    ratio = jnp.sqrt((total_in / D + epsilon) / (total_out / F + epsilon))
    damp_root = math.sqrt(damping)
    shift = ratio * damp_root if inward else damp_root / ratio
    c = [jnp.where(swapped, pltpu.roll(value, HALF, 1), value) for value in pieces]
    t = [jnp.concatenate([value, value], axis=0).T for value in c]
    low = lax.broadcasted_iota(jnp.int32, (HALF, LANES), 1) < HALF
    zero = jnp.zeros((HALF, LANES), jnp.float32)
    rows = [
        [c[0], jnp.where(low, c[1], zero)],
        [jnp.where(low, t[0][HALF:], c[1]), jnp.where(low, t[2][HALF:], zero)],
        [jnp.where(low, t[1][:HALF], c[2]), jnp.where(low, c[2], zero)],
        [zero, zero],
    ]
    blocks = jnp.concatenate([jnp.concatenate(pair, axis=1) for pair in rows], axis=0)
    i = lax.broadcasted_iota(jnp.int32, (256, 256), 0)
    j = lax.broadcasted_iota(jnp.int32, (256, 256), 1)
    identity = jnp.where((i == j) & (i < BLOCK), 1.0, 0.0).astype(jnp.float32)
    matrix = blocks * (1.0 / TOKENS) + shift * identity
    total = jnp.sum(matrix * matrix, axis=(0, 1), keepdims=True)
    iterate = identity / jnp.sqrt(total)
    for _ in range(STEPS):
        product = jnp.dot(matrix, iterate, precision=lax.Precision.HIGHEST, preferred_element_type=jnp.float32)
        iterate = jnp.dot(
            iterate, 2.0 * identity - product, precision=lax.Precision.HIGHEST, preferred_element_type=jnp.float32
        )
    return iterate[:BLOCK, :BLOCK].astype(jnp.bfloat16)


def inverse_in_kernel(index, one, two, out, trace_out):
    both = one[...] + two[...]
    trace = both[BLOCK:]
    trace_out[...] = trace
    pieces = [both[HALF * i : HALF * (i + 1)] for i in range(3)]
    out[...] = newton(pieces, trace, index[X_LOW_AT] == 1, True)


def inverse_out_kernel(index, trace, slots, out):
    both = (slots[0] + slots[1] + (slots[2] + slots[3])) + (slots[4] + slots[5] + (slots[6] + slots[7]))
    pieces = [both[HALF * i : HALF * (i + 1)] for i in range(3)]
    value = newton(pieces, trace[...], index[Y_LOW_AT] == 1, False)
    for i in range(8):
        out[i] = value


def inverse(kernel, index, args, shapes):
    vmem = pl.BlockSpec(memory_space=pltpu.VMEM)
    return pl.pallas_call(
        kernel,
        in_specs=[pl.BlockSpec(memory_space=pltpu.SMEM)] + [vmem] * len(args),
        out_specs=[vmem] * len(shapes),
        out_shape=[jax.ShapeDtypeStruct(*shape) for shape in shapes],
        cost_estimate=pl.CostEstimate(flops=5_000_000_000, bytes_accessed=200_000, transcendentals=0),
        compiler_params=pltpu.CompilerParams(vmem_limit_bytes=16 * MIB),
    )(index, *args)


def left_kernel(index, slots, weight, left, sums):
    for q in range(4):
        rows = slice(q * BLOCK, (q + 1) * BLOCK)
        left[rows, :] = jnp.dot(
            slots[index[LEFT_AT + q]], weight[rows, :], preferred_element_type=jnp.float32
        ).astype(jnp.bfloat16)
    for pair in range(4):
        at = 384 * pair
        turned = left[:, at : at + 384].T
        even = jnp.dot(turned[:BLOCK], weight[:, at : at + 256], preferred_element_type=jnp.float32)
        odd = jnp.dot(turned[BLOCK:], weight[:, at + 128 : at + 384], preferred_element_type=jnp.float32)
        sums[2 * pair] = even[:, :BLOCK]
        sums[2 * pair + 1] = odd[:, HALF:]


def left_product(index, slots, weight):
    vmem = pl.BlockSpec(memory_space=pltpu.VMEM)
    return pl.pallas_call(
        left_kernel,
        in_specs=[pl.BlockSpec(memory_space=pltpu.SMEM), vmem, vmem],
        out_specs=[vmem, vmem],
        out_shape=[
            jax.ShapeDtypeStruct(weight.shape, jnp.bfloat16),
            jax.ShapeDtypeStruct((8, BLOCK, BLOCK), jnp.float32),
        ],
        cost_estimate=pl.CostEstimate(flops=8_000_000_000, bytes_accessed=5_000_000, transcendentals=0),
        compiler_params=pltpu.CompilerParams(vmem_limit_bytes=24 * MIB),
        name="left",
    )(index, slots, weight)


def align_kernel(inverses, sums, total):
    product = jnp.zeros((BLOCK, BLOCK), jnp.float32)
    for block in range(8):
        product += inverses[block].astype(jnp.float32) * sums[block]
    total[...] = jnp.broadcast_to(jnp.sum(product, axis=(0, 1), keepdims=True), (128, LANES))


def align(inverses, sums):
    vmem = pl.BlockSpec(memory_space=pltpu.VMEM)
    return pl.pallas_call(
        align_kernel,
        in_specs=[vmem, vmem],
        out_specs=vmem,
        out_shape=jax.ShapeDtypeStruct((128, LANES), jnp.float32),
        cost_estimate=pl.CostEstimate(flops=500_000_000, bytes_accessed=1_500_000, transcendentals=0),
        compiler_params=pltpu.CompilerParams(vmem_limit_bytes=12 * MIB),
        name="align",
    )(inverses, sums)


def natural_kernel(left, inverses, totals, out):
    alignment = jnp.sum(totals[:, :1], axis=(0, 1), keepdims=True)
    scale = jnp.sqrt(trust_radius * D * F / alignment)
    zero = jnp.zeros((BLOCK, BLOCK), jnp.bfloat16)
    for pair in range(4):
        both = jnp.concatenate(
            [
                jnp.concatenate([inverses[2 * pair], zero], axis=1),
                jnp.concatenate([zero, inverses[2 * pair + 1]], axis=1),
            ],
            axis=0,
        )
        columns = slice(384 * pair, 384 * (pair + 1))
        natural = jnp.dot(left[:, columns], both, preferred_element_type=jnp.float32)
        out[:, columns] = (natural * scale).astype(jnp.bfloat16)


def natural_product(left, inverses, totals):
    vmem = pl.BlockSpec(memory_space=pltpu.VMEM)
    return pl.pallas_call(
        natural_kernel,
        in_specs=[vmem] * 3,
        out_specs=vmem,
        out_shape=jax.ShapeDtypeStruct(left.shape, jnp.bfloat16),
        cost_estimate=pl.CostEstimate(flops=3_000_000_000, bytes_accessed=10_000_000, transcendentals=0),
        compiler_params=pltpu.CompilerParams(vmem_limit_bytes=24 * MIB),
        name="natural",
    )(left, inverses, totals)


def side(far, at):
    return at // 2 if far else at % 2


def cubes(second):
    groups = {}
    for i in range(128):
        z, x_low, y, x_high, core = i // 32, i // 16 % 2, i // 4 % 4, i // 2 % 2, i % 2
        far = core == (0 if second else 1)
        axes = (z, 2 * x_high + x_low, y)
        rest = tuple(at % 2 ^ at // 2 if far else at // 2 for at in axes)
        order = tuple(side(far, at) for at in axes)
        groups.setdefault((core, rest), {})[order] = i
    return [[members[k] for k in sorted(members)] for members in groups.values()]


def trade(array, groups):
    return lax.all_to_all(array, ALL, split_axis=0, concat_axis=0, tiled=True, axis_index_groups=groups)


TOKENS_AT, GRADS_AT, OWN_AT, FIRST_AT, SECOND_AT = 0, 4, 20, 36, 44
Y_FIRST_AT, Y_SECOND_AT, Y_SLOT_AT, X_MOVED_AT, X_SECOND_AT = 52, 56, 60, 64, 68
LEFT_AT, IN_AT, X_LOW_AT, Y_LOW_AT = 72, 76, 77, 78


def index_table():
    table = np.zeros((128, 128), np.int32)
    for i in range(128):
        z, x_low, y, x_high, core = i // 32, i // 16 % 2, i // 4 % 4, i // 2 % 2, i % 2
        x = 2 * x_high + x_low

        def reached(c, at, last):
            near = 1 + 2 * c
            return [
                through if side(c == 0, through) == last else through ^ (4 - near) for through in (at, at ^ near)
            ]

        def moved(at, to):
            return int(at ^ to in (2, 1 + 2 * core))

        def through_side(at, to):
            return side(core == 1, at ^ (moved(at, to) * (1 + 2 * core)))

        def final_side(to):
            return side(core == 0, to)

        chunks = [(at * 2 + h) * 2 for last in range(2) for at in reached(1 - core, z, last) for h in range(2)]
        order = (x, x ^ (1 + 2 * x_low), x ^ (3 - 2 * x_low), x ^ 2)
        ring = range(4)
        rows = {
            TOKENS_AT: [1 - core],
            GRADS_AT: [at + 1 - core for at in chunks],
            OWN_AT: [
                ((at * 2 + to // 2) * 2 + core) * 2 + to % 2
                for last in range(2)
                for at in reached(core, z, last)
                for to in ring
            ],
            FIRST_AT: [
                4 * side(core == 1, through) + 2 * through_side(x, to)
                for through in (z, z ^ (1 + 2 * core))
                for to in ring
            ],
            SECOND_AT: [2 * final_side(to) for to in ring] * 2,
            Y_FIRST_AT: [through_side(y, to) for to in ring],
            Y_SECOND_AT: [final_side(to) for to in ring],
            Y_SLOT_AT: [2 * moved(y, to) + final_side(to) for to in ring],
            X_MOVED_AT: [moved(x, to) for to in ring],
            X_SECOND_AT: [final_side(to) for to in ring],
            LEFT_AT: [order.index(to) for to in ring],
            IN_AT: [4 * core],
            X_LOW_AT: [x_low],
            Y_LOW_AT: [y % 2],
        }
        for start, values in rows.items():
            table[i, start : start + len(values)] = values
    return table


def on_device(tokens, grads, weight_grad):
    x_low = lax.axis_index("row_0")
    y = lax.axis_index("row_1")
    x_high = lax.axis_index("col_0")
    core = lax.axis_index("col_1")
    index = lax.dynamic_index_in_dim(jnp.asarray(index_table()), lax.axis_index(ALL), 0, keepdims=False)

    half, trace = tokens_share(index, tokens)
    got_in = swap(half, 1, 1)
    one, two, trace = grads_share(index, grads, trace)
    got_trace = swap(trace, 1, 1)
    got_one = swap(one, 1, 1)
    got_two = swap(two, 1, 1)

    def pick(array, side_of, offset):
        at = jnp.where(core == 0, side_of // 2, lax.rem(side_of, 2)) ^ offset
        return lax.dynamic_index_in_dim(array, at, 0, keepdims=False)

    x = 2 * x_high + x_low
    send, keep = in_blocks(index, tokens, got_in, trace, got_trace)
    got = first(send, X_BITS)
    both = keep + got
    got = second(pick(both, x, 1), X_BITS)
    both = pick(both, x, 0) + got
    got = first(both[2:], Y_BITS)
    both = both[:2] + got
    got = second(pick(both, y, 1), Y_BITS)
    both = pick(both, y, 0) + got
    got = first(both, Z_BITS)
    both = both + got
    got = second(both, Z_BITS)
    own, trace = inverse(
        inverse_in_kernel, index, [both, got], [((BLOCK, BLOCK), jnp.bfloat16), ((8, LANES), jnp.float32)]
    )
    got = first(own, X_BITS)
    slots = jnp.stack([own, got])
    got = second(slots, X_BITS)
    slots = jnp.concatenate([slots, got], axis=0)
    got = swap(slots, 1, 1)
    slots = jnp.where(core == x_low, slots, got)
    left, sums = left_product(index, slots, weight_grad)

    parts = []
    for last, got in enumerate((got_one, got_two)):
        blocks = out_blocks(index, last, grads, got)
        blocks = trade((blocks * OUT_SCALE).astype(jnp.float16), cubes(False))
        parts.append(jnp.sum(blocks.astype(jnp.float32), axis=0) * (1.0 / OUT_SCALE))
    cube = jnp.concatenate(parts, axis=0)
    cube = trade(cube, cubes(True))
    (own,) = inverse(inverse_out_kernel, index, [trace, cube], [((8, BLOCK, BLOCK), jnp.bfloat16)])
    inverses = lax.all_to_all(own, ROW, split_axis=0, concat_axis=0, tiled=True)
    total = align(inverses, sums)
    totals = lax.all_to_all(total, ALL, split_axis=0, concat_axis=0, tiled=True)
    return natural_product(left, inverses, totals)


def solution(mesh):
    finer = Mesh(mesh.devices.reshape(mesh.shape["dp"], 2, 4, 2, 2), ALL)
    placed = (P(ALL, None), P(ALL, None), P(ROW, DP_COL))
    return jax.shard_map(on_device, mesh=finer, in_specs=placed, out_specs=P(ROW, DP_COL), check_vma=False)
```

time: 216 us -> 181 us (0.84)
  Pallas kernels: 68.8 us -> 51.1 us
  starting transfers between devices: 49.9 us -> 44.7 us
  blocking collectives: 23.7 us -> 19.6 us
  local copies, waits for them, and re-layouts: 9.59 us -> 6.66 us
  other arithmetic: 13.3 us -> 10.4 us
    ppermute x13, starting transfers between devices: 25.7 us -> 17 us  [swap(): lax.ppermute(array, ALL, [(i, i ^ (far if i % 2 else near)) for i in rang...]
    convert_element_type x0 -> x2, other arithmetic: none -> 6.94 us  [on_device(): blocks = trade((blocks * OUT_SCALE).astype(jnp.float16), cubes(False))]
    pallas_call x1, Pallas kernels: 16.8 us -> 10.1 us  [grads_share(): pl.pallas_call(grads_kernel, grid_spec=pltpu.PrefetchScalarGridSpec(num_s...]
    all_to_all x1, blocking collectives: 23.7 us -> 19.6 us  [on_device(): totals = lax.all_to_all(total, ALL, split_axis=0, concat_axis=0, tiled=True)]
    pallas_call x1, Pallas kernels: 6.25 us -> 3.6 us  [in_blocks(): pl.pallas_call(in_kernel, grid_spec=pltpu.PrefetchScalarGridSpec(num_scal...]
    another operation x4 -> x0, local copies, waits for them, and re-layouts: 2.59 us -> none  [ints(): return jnp.stack([jnp.asarray(v, jnp.int32) for v in values])]
    pallas_call x1, Pallas kernels: 4.51 us -> 1.99 us  [left_product(): pl.pallas_call(left_kernel, in_specs=[pl.BlockSpec(memory_space=pltpu.SME...]
    pallas_call x1, Pallas kernels: 2.6 us -> 0.34 us  [align(): pl.pallas_call(align_kernel, in_specs=[vmem, vmem], out_specs=vmem, out_s...]
  transfers between devices with their start and end apart: 17 -> 17, of which waited for: 10 -> 11; matrix products, arithmetic and copies ran while one was open for 7% -> 6% of each run, Pallas kernels for 16% -> 21%
where the time goes in v1:
time: 181 us; the launch traced here: 180 us
  Pallas kernels  51.1 us (28%)
  waiting for transfers between devices  47.8 us (26%)
  starting transfers between devices  44.7 us (25%)
  blocking collectives  19.6 us (11%)
  other arithmetic  10.4 us (6%)
  local copies, waits for them, and re-layouts  6.66 us (4%)
    ppermute x13, waiting for transfers between devices, swap(): lax.ppermute(array, ALL, [(i, i ^ (far if i % 2 else near)) for i in rang...  37.2 us
    all_to_all x3, starting transfers between devices, trade(): lax.all_to_all(array, ALL, split_axis=0, concat_axis=0, tiled=True, axis_...  21.9 us
    all_to_all x1, blocking collectives, on_device(): totals = lax.all_to_all(total, ALL, split_axis=0, concat_axis=0, tiled=True)  19.6 us
    pallas_call x2, Pallas kernels, out_blocks(): pl.pallas_call(out_kernel, grid_spec=pltpu.PrefetchScalarGridSpec(num_sca...  18.5 us
    ppermute x13, starting transfers between devices, swap(): lax.ppermute(array, ALL, [(i, i ^ (far if i % 2 else near)) for i in rang...  17 us
    pallas_call x1, Pallas kernels, grads_share(): pl.pallas_call(grads_kernel, grid_spec=pltpu.PrefetchScalarGridSpec(num_s...  10.1 us
    pallas_call x2, Pallas kernels, inverse(): pl.pallas_call(kernel, in_specs=[pl.BlockSpec(memory_space=pltpu.SMEM)] +...  9.03 us
    all_to_all x3, waiting for transfers between devices, trade(): lax.all_to_all(array, ALL, split_axis=0, concat_axis=0, tiled=True, axis_...  7.38 us
  transfers between devices with their start and end apart: 17, of which 11 were waited for; matrix products, arithmetic and copies ran while one was open for 6% of the time, Pallas kernels for 21%

profile of v1, /device:TPU:1, one launch (start us, length us, event | category | flops | bytes accessed | tf_op | source)
XLA Modules:
  0.0 180.5 jit_solution(9315037572282010714)
XLA Ops:
  1.2 4.6 %tokens_share.1 = (bf16[256,3072]{1,0:T(8,128)(2,1)}, f32[8,128]{1,0:T(8,128)}) custom-call(s32[128]{0:T(128)} %fusion.index, bf16[256,6144]{1,0:T(8,128)(2,1)} %own.3), custom_call_target="tpu_custom_call" | custom-call | flops 500000000 | bytes 5000000 | tf_op jit(solution)/shard_map/tokens_share/pallas_call | solution.py:164
  7.1 10.1 %grads_share.1 = (bf16[256,6144]{1,0:T(8,128)(2,1)}, bf16[256,6144]{1,0:T(8,128)(2,1)}, f32[8,128]{1,0:T(8,128)}) custom-call(s32[128]{0:T(128)} %fusion.index, bf16[256,24576]{1,0:T(8,128)(2,1)} %own.5, f32[8,128]{1,0:T(8,128)} %get-tuple-element.17.before), custom_call_target="tpu_custom_call" | custom-call | flops 2000000000 | bytes 20000000 | tf_op jit(solution)/shard_map/grads_share/pallas_call | solution.py:199
  17.8 5.5 %collective-permute-done.1.trace_got = f32[8,128]{1,0:T(8,128)S(1)} collective-permute-done((f32[8,128]{1,0:T(8,128)}, f32[8,128]{1,0:T(8,128)S(1)}, u32[]{:S(2)}, u32[]{:S(2)}) %collective-permute-start.1) | collective-permute-done | bytes 4128 | tf_op jit(solution)/shard_map/ppermute | solution.py:39
  24.0 3.6 %cov_in.1 = (f32[2,4,200,128]{3,2,1,0:T(8,128)S(1)}, f32[2,4,200,128]{3,2,1,0:T(8,128)S(1)}) custom-call(s32[128]{0:T(128)S(1)} %copy-done.1, bf16[256,6144]{1,0:T(8,128)(2,1)S(1)} %copy-done, bf16[256,3072]{1,0:T(8,128)(2,1)S(1)} %collective-permute-done.got, f32[8,128]{1,0:T(8,128)S(1)} %copy-done.4, f32[8,128]{1,0:T(8,128)S(1)} %collective-permute-done.1.trace_got), custom_call_target="tpu_custom_call" | custom-call | flops 5000000000 | bytes 5000000 | tf_op jit(solution)/shard_map/cov_in/pallas_call | solution.py:120
  30.2 9.8 %collective-permute-done.2 = f32[2,4,200,128]{3,2,1,0:T(8,128)S(1)} collective-permute-done((f32[2,4,200,128]{3,2,1,0:T(8,128)S(1)}, f32[2,4,200,128]{3,2,1,0:T(8,128)S(1)}, u32[]{:S(2)}, u32[]{:S(2)}) %collective-permute-start.2) | collective-permute-done | bytes 819232 | tf_op jit(solution)/shard_map/ppermute | solution.py:39
  40.7 6.7 %collective-permute-done.3 = f32[4,200,128]{2,1,0:T(8,128)S(1)} collective-permute-done((f32[4,200,128]{2,1,0:T(8,128)S(1)}, f32[4,200,128]{2,1,0:T(8,128)S(1)}, u32[]{:S(2)}, u32[]{:S(2)}) %collective-permute-start.3) | collective-permute-done | bytes 409632 | tf_op jit(solution)/shard_map/ppermute | solution.py:39
  50.4 3.1 %collective-permute-done.4 = f32[2,200,128]{2,1,0:T(8,128)S(1)} collective-permute-done((f32[2,200,128]{2,1,0:T(8,128)S(1)}, f32[2,200,128]{2,1,0:T(8,128)S(1)}, u32[]{:S(2)}, u32[]{:S(2)}) %collective-permute-start.4) | collective-permute-done | bytes 204832 | tf_op jit(solution)/shard_map/ppermute | solution.py:39
  53.6 9.3 %cov_out.2 = f32[8,4,192,128]{3,2,1,0:T(8,128)} custom-call(s32[128]{0:T(128)} %fusion.index, bf16[256,24576]{1,0:T(8,128)(2,1)} %own.5, bf16[256,6144]{1,0:T(8,128)(2,1)} %collective-permute-done.11.got), custom_call_target="tpu_custom_call" | custom-call | flops 10000000000 | bytes 10000000 | tf_op jit(solution)/shard_map/cov_out/pallas_call | solution.py:81
  62.8 3.5 %multiply_convert_fusion.1 = f16[8,4,192,128]{3,2,1,0:T(8,128)(2,1)} fusion(f32[8,4,192,128]{3,2,1,0:T(8,128)} %cov_out.2), kind=kLoop, calls=%fused_computation.3 | loop fusion | flops 1572864 | bytes 4718592 | tf_op jit(solution)/shard_map/convert_element_type | solution.py:486
  66.3 9.6 %all-to-all-start = ((f16[8,4,192,128]{3,2,1,0:T(8,128)(2,1)}), f16[8,4,192,128]{3,2,1,0:T(8,128)(2,1)S(1)}, u32[]{:S(2)}, u32[]{:S(2)}) async-start(f16[8,4,192,128]{3,2,1,0:T(8,128)(2,1)} %multiply_convert_fusion.1), calls=%async_computation | async-start | bytes 3145728 | tf_op jit(solution)/shard_map/all_to_all | solution.py:379
  76.0 9.2 %cov_out.3 = f32[8,4,192,128]{3,2,1,0:T(8,128)} custom-call(s32[128]{0:T(128)} %fusion.index, bf16[256,24576]{1,0:T(8,128)(2,1)} %own.5, bf16[256,6144]{1,0:T(8,128)(2,1)} %collective-permute-done.12.got), custom_call_target="tpu_custom_call" | custom-call | flops 10000000000 | bytes 10000000 | tf_op jit(solution)/shard_map/cov_out/pallas_call | solution.py:81
  85.2 3.5 %multiply_convert_fusion = f16[8,4,192,128]{3,2,1,0:T(8,128)(2,1)} fusion(f32[8,4,192,128]{3,2,1,0:T(8,128)} %cov_out.3), kind=kLoop, calls=%fused_computation.1 | loop fusion | flops 1572864 | bytes 4718592 | tf_op jit(solution)/shard_map/convert_element_type | solution.py:486
  88.7 3.7 %all-to-all-done = f16[8,4,192,128]{3,2,1,0:T(8,128)(2,1)S(1)} async-done(((f16[8,4,192,128]{3,2,1,0:T(8,128)(2,1)}), f16[8,4,192,128]{3,2,1,0:T(8,128)(2,1)S(1)}, u32[]{:S(2)}, u32[]{:S(2)}) %all-to-all-start) | async-done | bytes 1572896 | tf_op jit(solution)/shard_map/all_to_all | solution.py:379
  92.4 4.4 %all-to-all-start.1 = ((f16[8,4,192,128]{3,2,1,0:T(8,128)(2,1)}), f16[8,4,192,128]{3,2,1,0:T(8,128)(2,1)S(1)}, u32[]{:S(2)}, u32[]{:S(2)}) async-start(f16[8,4,192,128]{3,2,1,0:T(8,128)(2,1)} %multiply_convert_fusion), calls=%async_computation.1 | async-start | bytes 3145728 | tf_op jit(solution)/shard_map/all_to_all | solution.py:379
  100.5 3.5 %collective-permute-done.6 = f32[200,128]{1,0:T(8,128)S(1)} collective-permute-done((f32[200,128]{1,0:T(8,128)S(1)}, f32[200,128]{1,0:T(8,128)S(1)}, u32[]{:S(2)}, u32[]{:S(2)}) %collective-permute-start.6) | collective-permute-done | bytes 102432 | tf_op jit(solution)/shard_map/ppermute | solution.py:39
  104.2 4.3 %collective-permute-done.7.two = f32[200,128]{1,0:T(8,128)S(1)} collective-permute-done((f32[200,128]{1,0:T(8,128)S(1)}, f32[200,128]{1,0:T(8,128)S(1)}, u32[]{:S(2)}, u32[]{:S(2)}) %collective-permute-start.7) | collective-permute-done | bytes 102432 | tf_op jit(solution)/shard_map/ppermute | solution.py:39
  108.4 4.1 %shard_map.46 = (bf16[192,192]{1,0:T(8,128)(2,1)S(1)}, f32[8,128]{1,0:T(8,128)S(1)}) custom-call(s32[128]{0:T(128)S(1)} %copy-done.2, f32[200,128]{1,0:T(8,128)S(1)} %add.64.one, f32[200,128]{1,0:T(8,128)S(1)} %collective-permute-done.7.two), custom_call_target="tpu_custom_call" | custom-call | flops 5000000000 | bytes 200000 | tf_op jit(solution)/shard_map/pallas_call | solution.py:271
  120.0 7.9 %all-to-all-start.2 = ((f32[8,192,128]{2,1,0:T(8,128)}), f32[8,192,128]{2,1,0:T(8,128)S(1)}, u32[]{:S(2)}, u32[]{:S(2)}) async-start(f32[8,192,128]{2,1,0:T(8,128)} %pad_maximum_fusion), calls=%async_computation.2 | async-start | bytes 1572864 | tf_op jit(solution)/shard_map/all_to_all | solution.py:379
  128.0 3.7 %collective-permute-start.10 = (bf16[4,192,192]{2,1,0:T(8,128)(2,1)S(1)}, bf16[4,192,192]{2,1,0:T(8,128)(2,1)S(1)}, u32[]{:S(2)}, u32[]{:S(2)}) collective-permute-start(bf16[4,192,192]{2,1,0:T(8,128)(2,1)S(1)} %pad_maximum_fusion.1), channel_id=1, source_target_pairs={{0,1},{1,0},{2,3},{3,2},{4,5},{5,4},{6,7},{7,6},{8,9},{9,8},{10,11... | collective-permute-start | bytes 884744 | tf_op jit(solution)/shard_map/ppermute | solution.py:39
  133.2 3.6 %all-to-all-done.2.slots = f32[8,192,128]{2,1,0:T(8,128)S(1)} async-done(((f32[8,192,128]{2,1,0:T(8,128)}), f32[8,192,128]{2,1,0:T(8,128)S(1)}, u32[]{:S(2)}, u32[]{:S(2)}) %all-to-all-start.2) | async-done | bytes 786464 | tf_op jit(solution)/shard_map/all_to_all | solution.py:379
  136.8 5.0 %shard_map.47 = bf16[8,192,192]{2,1,0:T(8,128)(2,1)} custom-call(s32[128]{0:T(128)S(1)} %copy-done.2, f32[8,128]{1,0:T(8,128)S(1)} %get-tuple-element.23.trace, f32[8,192,128]{2,1,0:T(8,128)S(1)} %all-to-all-done.2.slots), custom_call_target="tpu_custom_call" | custom-call | flops 5000000000 | bytes 200000 | tf_op jit(solution)/shard_map/pallas_call | solution.py:271
  141.7 5.8 %all-to-all-start.3 = ((bf16[8,192,192]{2,1,0:T(8,128)(2,1)}), bf16[8,192,192]{2,1,0:T(8,128)(2,1)S(1)}, u32[]{:S(2)}, u32[]{:S(2)}) async-start(bf16[8,192,192]{2,1,0:T(8,128)(2,1)} %shard_map.47), calls=%async_computation.3 | async-start | bytes 1572864 | tf_op jit(solution)/shard_map/all_to_all | solution.py:491
  152.6 3.3 %all-to-all-done.3.inverses = bf16[8,192,192]{2,1,0:T(8,128)(2,1)S(1)} async-done(((bf16[8,192,192]{2,1,0:T(8,128)(2,1)}), bf16[8,192,192]{2,1,0:T(8,128)(2,1)S(1)}, u32[]{:S(2)}, u32[]{:S(2)}) %all-to-all-start.3) | async-done | bytes 589856 | tf_op jit(solution)/shard_map/all_to_all | solution.py:491
  156.2 19.6 %all_to_all.31 = f32[128,1,128]{2,1,0:T(1,128)S(1)} all-to-all(f32[128,1,128]{2,1,0:T(1,128)S(1)} %bitcast.19), channel_id=1, replica_groups=mesh['dp'=4,'row_0'=2,'row_1'=4,'col_0'=2,'col_1'=2] {'dp','row_0','row_..., dimensions={0} | all-to-all | bytes 131072 | tf_op jit(solution)/shard_map/all_to_all | solution.py:493
  (54 shorter events, 33.1 us)
Async XLA Ops:
  5.8 17.5 %collective-permute-start = (bf16[256,3072]{1,0:T(8,128)(2,1)}, bf16[256,3072]{1,0:T(8,128)(2,1)S(1)}, u32[]{:S(2)}, u32[]{:S(2)}) collective-permute-start(bf16[256,3072]{1,0:T(8,128)(2,1)} %get-tuple-element.16), channel_id=1, source_target_pairs={{0,1},{1,0},{2,3},{3,2},{4,5},{5,4},{6,7},{7,6},{8,9},{9,8},{10,11... | collective-permute-start | bytes 4718600 | tf_op jit(solution)/shard_map/ppermute | solution.py:39
  7.1 16.1 %copy-start = (bf16[256,6144]{1,0:T(8,128)(2,1)S(1)}, bf16[256,6144]{1,0:T(8,128)(2,1)}, u32[]{:S(2)}) copy-start(bf16[256,6144]{1,0:T(8,128)(2,1)} %own.3) | copy-start | bytes 9437188
  7.1 16.1 %copy-start.1 = (s32[128]{0:T(128)S(1)}, s32[128]{0:T(128)}, u32[]{:S(2)}) copy-start(s32[128]{0:T(128)} %fusion.index) | copy-start | bytes 1540
  17.2 36.3 %collective-permute-start.11 = (bf16[256,6144]{1,0:T(8,128)(2,1)}, bf16[256,6144]{1,0:T(8,128)(2,1)}, u32[]{:S(2)}, u32[]{:S(2)}) collective-permute-start(bf16[256,6144]{1,0:T(8,128)(2,1)} %get-tuple-element.24), channel_id=1, source_target_pairs={{0,1},{1,0},{2,3},{3,2},{4,5},{5,4},{6,7},{7,6},{8,9},{9,8},{10,11... | collective-permute-start | bytes 9437192 | tf_op jit(solution)/shard_map/ppermute | solution.py:39
  17.3 6.0 %collective-permute-start.1 = (f32[8,128]{1,0:T(8,128)}, f32[8,128]{1,0:T(8,128)S(1)}, u32[]{:S(2)}, u32[]{:S(2)}) collective-permute-start(f32[8,128]{1,0:T(8,128)} %get-tuple-element.18.trace_own), channel_id=1, source_target_pairs={{0,1},{1,0},{2,3},{3,2},{4,5},{5,4},{6,7},{7,6},{8,9},{9,8},{10,11... | collective-permute-start | bytes 12296 | tf_op jit(solution)/shard_map/ppermute | solution.py:39
  23.3 0.7 copy-start.4
  27.6 12.5 %collective-permute-start.2 = (f32[2,4,200,128]{3,2,1,0:T(8,128)S(1)}, f32[2,4,200,128]{3,2,1,0:T(8,128)S(1)}, u32[]{:S(2)}, u32[]{:S(2)}) collective-permute-start(f32[2,4,200,128]{3,2,1,0:T(8,128)S(1)} %get-tuple-element.20), channel_id=1, source_target_pairs={{0,16},{1,19},{2,18},{3,17},{4,20},{5,23},{6,22},{7,21},{8,24},{9,... | collective-permute-start | bytes 2457608 | tf_op jit(solution)/shard_map/ppermute | solution.py:39
  30.2 45.8 %collective-permute-start.12 = (bf16[256,6144]{1,0:T(8,128)(2,1)}, bf16[256,6144]{1,0:T(8,128)(2,1)}, u32[]{:S(2)}, u32[]{:S(2)}) collective-permute-start(bf16[256,6144]{1,0:T(8,128)(2,1)} %get-tuple-element.25), channel_id=1, source_target_pairs={{0,1},{1,0},{2,3},{3,2},{4,5},{5,4},{6,7},{7,6},{8,9},{9,8},{10,11... | collective-permute-start | bytes 9437192 | tf_op jit(solution)/shard_map/ppermute | solution.py:39
  40.2 7.2 %collective-permute-start.3 = (f32[4,200,128]{2,1,0:T(8,128)S(1)}, f32[4,200,128]{2,1,0:T(8,128)S(1)}, u32[]{:S(2)}, u32[]{:S(2)}) collective-permute-start(f32[4,200,128]{2,1,0:T(8,128)S(1)} %dynamic-slice_bitcast_fusion), channel_id=1, source_target_pairs={{0,18},{1,17},{2,16},{3,19},{4,22},{5,21},{6,20},{7,23},{8,26},{9,... | collective-permute-start | bytes 1228808 | tf_op jit(solution)/shard_map/ppermute | solution.py:39
  47.4 6.1 %collective-permute-start.4 = (f32[2,200,128]{2,1,0:T(8,128)S(1)}, f32[2,200,128]{2,1,0:T(8,128)S(1)}, u32[]{:S(2)}, u32[]{:S(2)}) collective-permute-start(f32[2,200,128]{2,1,0:T(8,128)S(1)} %slice.9), channel_id=1, source_target_pairs={{0,4},{1,13},{2,6},{3,15},{4,0},{5,9},{6,2},{7,11},{8,12},{9,5},{1... | collective-permute-start | bytes 614408 | tf_op jit(solution)/shard_map/ppermute | solution.py:39
  66.3 26.1 %all-to-all-start = ((f16[8,4,192,128]{3,2,1,0:T(8,128)(2,1)}), f16[8,4,192,128]{3,2,1,0:T(8,128)(2,1)S(1)}, u32[]{:S(2)}, u32[]{:S(2)}) async-start(f16[8,4,192,128]{3,2,1,0:T(8,128)(2,1)} %multiply_convert_fusion.1), calls=%async_computation | async-start | bytes 3145728 | tf_op jit(solution)/shard_map/all_to_all | solution.py:379
  75.9 20.9 %collective-permute-start.5 = (f32[200,128]{1,0:T(8,128)S(1)}, f32[200,128]{1,0:T(8,128)}, u32[]{:S(2)}, u32[]{:S(2)}) collective-permute-start(f32[200,128]{1,0:T(8,128)S(1)} %dynamic-slice_bitcast_fusion.1), channel_id=1, source_target_pairs={{0,12},{1,5},{2,14},{3,7},{4,8},{5,1},{6,10},{7,3},{8,4},{9,13},{1... | collective-permute-start | bytes 307208 | tf_op jit(solution)/shard_map/ppermute | solution.py:39
  85.2 23.2 %copy-start.2 = (s32[128]{0:T(128)S(1)}, s32[128]{0:T(128)}, u32[]{:S(2)}) copy-start(s32[128]{0:T(128)} %fusion.index) | copy-start | bytes 1540
  92.4 26.4 %all-to-all-start.1 = ((f16[8,4,192,128]{3,2,1,0:T(8,128)(2,1)}), f16[8,4,192,128]{3,2,1,0:T(8,128)(2,1)S(1)}, u32[]{:S(2)}, u32[]{:S(2)}) async-start(f16[8,4,192,128]{3,2,1,0:T(8,128)(2,1)} %multiply_convert_fusion), calls=%async_computation.1 | async-start | bytes 3145728 | tf_op jit(solution)/shard_map/all_to_all | solution.py:379
  97.8 6.3 %collective-permute-start.6 = (f32[200,128]{1,0:T(8,128)S(1)}, f32[200,128]{1,0:T(8,128)S(1)}, u32[]{:S(2)}, u32[]{:S(2)}) collective-permute-start(f32[200,128]{1,0:T(8,128)S(1)} %bitcast_add_fusion.1), channel_id=1, source_target_pairs={{0,32},{1,97},{2,34},{3,99},{4,36},{5,101},{6,38},{7,103},{8,40},{... | collective-permute-start | bytes 307208 | tf_op jit(solution)/shard_map/ppermute | solution.py:39
  104.1 4.4 %collective-permute-start.7 = (f32[200,128]{1,0:T(8,128)S(1)}, f32[200,128]{1,0:T(8,128)S(1)}, u32[]{:S(2)}, u32[]{:S(2)}) collective-permute-start(f32[200,128]{1,0:T(8,128)S(1)} %add.64.one), channel_id=1, source_target_pairs={{0,96},{1,33},{2,98},{3,35},{4,100},{5,37},{6,102},{7,39},{8,104},... | collective-permute-start | bytes 307208 | tf_op jit(solution)/shard_map/ppermute | solution.py:39
  112.5 4.8 %collective-permute-start.8 = (bf16[192,192]{1,0:T(8,128)(2,1)S(1)}, bf16[192,192]{1,0:T(8,128)(2,1)S(1)}, u32[]{:S(2)}, u32[]{:S(2)}) collective-permute-start(bf16[192,192]{1,0:T(8,128)(2,1)S(1)} %get-tuple-element.21), channel_id=1, source_target_pairs={{0,16},{1,19},{2,18},{3,17},{4,20},{5,23},{6,22},{7,21},{8,24},{9,... | collective-permute-start | bytes 221192 | tf_op jit(solution)/shard_map/ppermute | solution.py:39
  118.0 10.0 %collective-permute-start.9 = (bf16[2,192,192]{2,1,0:T(8,128)(2,1)}, bf16[2,192,192]{2,1,0:T(8,128)(2,1)S(1)}, u32[]{:S(2)}, u32[]{:S(2)}) collective-permute-start(bf16[2,192,192]{2,1,0:T(8,128)(2,1)} %pad_maximum_fusion.2), channel_id=1, source_target_pairs={{0,18},{1,17},{2,16},{3,19},{4,22},{5,21},{6,20},{7,23},{8,26},{9,... | collective-permute-start | bytes 442376 | tf_op jit(solution)/shard_map/ppermute | solution.py:39
  120.0 16.7 %all-to-all-start.2 = ((f32[8,192,128]{2,1,0:T(8,128)}), f32[8,192,128]{2,1,0:T(8,128)S(1)}, u32[]{:S(2)}, u32[]{:S(2)}) async-start(f32[8,192,128]{2,1,0:T(8,128)} %pad_maximum_fusion), calls=%async_computation.2 | async-start | bytes 1572864 | tf_op jit(solution)/shard_map/all_to_all | solution.py:379
  128.0 5.0 %collective-permute-start.10 = (bf16[4,192,192]{2,1,0:T(8,128)(2,1)S(1)}, bf16[4,192,192]{2,1,0:T(8,128)(2,1)S(1)}, u32[]{:S(2)}, u32[]{:S(2)}) collective-permute-start(bf16[4,192,192]{2,1,0:T(8,128)(2,1)S(1)} %pad_maximum_fusion.1), channel_id=1, source_target_pairs={{0,1},{1,0},{2,3},{3,2},{4,5},{5,4},{6,7},{7,6},{8,9},{9,8},{10,11... | collective-permute-start | bytes 884744 | tf_op jit(solution)/shard_map/ppermute | solution.py:39
  141.7 14.1 %all-to-all-start.3 = ((bf16[8,192,192]{2,1,0:T(8,128)(2,1)}), bf16[8,192,192]{2,1,0:T(8,128)(2,1)S(1)}, u32[]{:S(2)}, u32[]{:S(2)}) async-start(bf16[8,192,192]{2,1,0:T(8,128)(2,1)} %shard_map.47), calls=%async_computation.3 | async-start | bytes 1572864 | tf_op jit(solution)/shard_map/all_to_all | solution.py:491
  147.5 1.7 copy-start.3
  151.2 1.4 copy-start.5
  175.7 1.7 copy-start.6

commit v2 on v1

--- a/solution.py
+++ b/solution.py
@@ -63,10 +63,27 @@
     return evens, odds
 
 
-def out_kernel(index, own, got, out):
+def out_kernel(base, index, own, got, out, own_held, got_held, own_sems, got_sems):
     step = pl.program_id(0)
+
+    def own_copy(i):
+        at = pl.multiple_of(index[base + i] * 768, 768)
+        return pltpu.make_async_copy(own.at[:, pl.ds(at, 768)], own_held.at[i], own_sems.at[i])
+
+    def got_copy(i):
+        at = pl.multiple_of(i * 768, 768)
+        return pltpu.make_async_copy(got.at[:, pl.ds(at, 768)], got_held.at[i], got_sems.at[i])
+
+    @pl.when(step == 0)
+    def _():
+        for i in range(8):
+            own_copy(i).start()
+            got_copy(i).start()
+
+    own_copy(step).wait()
+    got_copy(step).wait()
     for pair in range(2):
-        pieces = packed_pair(own, got, pair * 384)
+        pieces = packed_pair(own_held.at[step], got_held.at[step], pair * 384)
         for parity in range(2):
             at = 2 * pair + parity
             first = index[FIRST_AT + step] + index[Y_FIRST_AT + at]
@@ -77,21 +94,23 @@
 
 def out_blocks(index, last, own, got):
     shape = (8, 4, BLOCK, LANES)
-    base = OWN_AT + 8 * last
-    return pl.pallas_call(
-        out_kernel,
+    return pl.pallas_call(
+        functools.partial(out_kernel, OWN_AT + 8 * last),
         grid_spec=pltpu.PrefetchScalarGridSpec(
             num_scalar_prefetch=1,
             grid=(8,),
-            in_specs=[
-                pl.BlockSpec((256, 768), lambda i, w: (0, w[base + i])),
-                pl.BlockSpec((256, 768), lambda i, w: (0, i)),
+            in_specs=[pl.BlockSpec(memory_space=pl.ANY)] * 2,
+            out_specs=pl.BlockSpec(shape, lambda i, w: (0, 0, 0, 0)),
+            scratch_shapes=[
+                pltpu.VMEM((8, 256, 768), jnp.bfloat16),
+                pltpu.VMEM((8, 256, 768), jnp.bfloat16),
+                pltpu.SemaphoreType.DMA((8,)),
+                pltpu.SemaphoreType.DMA((8,)),
             ],
-            out_specs=pl.BlockSpec(shape, lambda i, w: (0, 0, 0, 0)),
         ),
         out_shape=jax.ShapeDtypeStruct(shape, jnp.float32),
         cost_estimate=pl.CostEstimate(flops=10_000_000_000, bytes_accessed=10_000_000, transcendentals=0),
-        compiler_params=pltpu.CompilerParams(vmem_limit_bytes=56 * MIB),
+        compiler_params=pltpu.CompilerParams(vmem_limit_bytes=54 * MIB),
         name="cov_out",
     )(index, own, got)
 
@@ -150,73 +169,52 @@
     return total[:4] + total[4:]
 
 
-def tokens_kernel(index, tokens, out, total):
-    @pl.when(pl.program_id(0) == 0)
-    def _():
-        total[...] = jnp.zeros_like(total)
-
-    at = pl.multiple_of(index[TOKENS_AT] * (D // 2), D // 2)
-    out[...] = tokens[:, pl.ds(at, D // 2)]
-    total[:4] += squares_of(tokens)
-
-
-def tokens_share(index, tokens):
-    return pl.pallas_call(
-        tokens_kernel,
-        grid_spec=pltpu.PrefetchScalarGridSpec(
-            num_scalar_prefetch=1,
-            grid=(4,),
-            in_specs=[pl.BlockSpec((64, D), lambda i, w: (i, 0))],
-            out_specs=[
-                pl.BlockSpec((64, D // 2), lambda i, w: (i, 0)),
-                pl.BlockSpec((8, LANES), lambda i, w: (0, 0)),
-            ],
-        ),
-        out_shape=[
-            jax.ShapeDtypeStruct((256, D // 2), jnp.bfloat16),
-            jax.ShapeDtypeStruct((8, LANES), jnp.float32),
+def share_kernel(chunk, first, count, index, array, *refs):
+    outs, (total, held, in_sems, out_sems) = refs[:-4], refs[-4:]
+    steps, rows = 8, 32
+    each = count // len(outs)
+
+    def in_copy(i):
+        where = pl.ds(i * rows, rows)
+        return pltpu.make_async_copy(array.at[where], held.at[where], in_sems.at[i])
+
+    def out_copy(i, j):
+        where = pl.ds(i * rows, rows)
+        at = pl.multiple_of(index[first + j] * chunk, chunk)
+        to = outs[j // each].at[where, pl.ds(j % each * chunk, chunk)]
+        return pltpu.make_async_copy(held.at[where, pl.ds(at, chunk)], to, out_sems.at[i, j])
+
+    for i in range(steps):
+        in_copy(i).start()
+    total[...] = jnp.zeros_like(total)
+    for i in range(steps):
+        in_copy(i).wait()
+        for j in range(count):
+            out_copy(i, j).start()
+        total[...] += squares_of(held.at[pl.ds(i * rows, rows)])
+    for i in range(steps):
+        for j in range(count):
+            out_copy(i, j).wait()
+
+
+def share(index, array, chunk, first, count, parts):
+    width = array.shape[1]
+    vmem = pl.BlockSpec(memory_space=pltpu.VMEM)
+    anywhere = pl.BlockSpec(memory_space=pl.ANY)
+    return pl.pallas_call(
+        functools.partial(share_kernel, chunk, first, count),
+        in_specs=[pl.BlockSpec(memory_space=pltpu.SMEM), anywhere],
+        out_specs=[anywhere] * parts + [vmem],
+        out_shape=[jax.ShapeDtypeStruct((256, chunk * count // parts), jnp.bfloat16)] * parts
+        + [jax.ShapeDtypeStruct((4, LANES), jnp.float32)],
+        scratch_shapes=[
+            pltpu.VMEM((256, width), jnp.bfloat16),
+            pltpu.SemaphoreType.DMA((8,)),
+            pltpu.SemaphoreType.DMA((8, count)),
         ],
-        cost_estimate=pl.CostEstimate(flops=500_000_000, bytes_accessed=5_000_000, transcendentals=0),
+        cost_estimate=pl.CostEstimate(flops=2_000_000_000, bytes_accessed=20_000_000, transcendentals=0),
         compiler_params=pltpu.CompilerParams(vmem_limit_bytes=60 * MIB),
-        name="tokens_share",
-    )(index, tokens)
-
-
-def grads_kernel(index, grads, before, one, two, total):
-    @pl.when(pl.program_id(0) == 0)
-    def _():
-        total[...] = before[...]
-
-    for chunk in range(4):
-        for half, out in enumerate((one, two)):
-            at = pl.multiple_of(index[GRADS_AT + 4 * half + chunk] * 1536, 1536)
-            out[:, 1536 * chunk : 1536 * (chunk + 1)] = grads[:, pl.ds(at, 1536)]
-    total[4:] += squares_of(grads)
-
-
-def grads_share(index, grads, before):
-    rows = 32
-    return pl.pallas_call(
-        grads_kernel,
-        grid_spec=pltpu.PrefetchScalarGridSpec(
-            num_scalar_prefetch=1,
-            grid=(256 // rows,),
-            in_specs=[
-                pl.BlockSpec((rows, F), lambda i, w: (i, 0)),
-                pl.BlockSpec((8, LANES), lambda i, w: (0, 0)),
-            ],
-            out_specs=[
-                pl.BlockSpec((rows, 6144), lambda i, w: (i, 0)),
-                pl.BlockSpec((rows, 6144), lambda i, w: (i, 0)),
-                pl.BlockSpec((8, LANES), lambda i, w: (0, 0)),
-            ],
-        ),
-        out_shape=[jax.ShapeDtypeStruct((256, 6144), jnp.bfloat16)] * 2
-        + [jax.ShapeDtypeStruct((8, LANES), jnp.float32)],
-        cost_estimate=pl.CostEstimate(flops=2_000_000_000, bytes_accessed=20_000_000, transcendentals=0),
-        compiler_params=pltpu.CompilerParams(vmem_limit_bytes=56 * MIB),
-        name="grads_share",
-    )(index, grads, before)
+    )(index, array)
 
 
 def newton(pieces, trace, swapped, inward):
@@ -250,8 +248,8 @@
     return iterate[:BLOCK, :BLOCK].astype(jnp.bfloat16)
 
 
-def inverse_in_kernel(index, one, two, out, trace_out):
-    both = one[...] + two[...]
+def inverse_in_kernel(index, one, two, three, four, out, trace_out):
+    both = (one[...] + three[...]) + (two[...] + four[...])
     trace = both[BLOCK:]
     trace_out[...] = trace
     pieces = [both[HALF * i : HALF * (i + 1)] for i in range(3)]
@@ -406,7 +404,6 @@
             return side(core == 0, to)
 
         chunks = [(at * 2 + h) * 2 for last in range(2) for at in reached(1 - core, z, last) for h in range(2)]
-        order = (x, x ^ (1 + 2 * x_low), x ^ (3 - 2 * x_low), x ^ 2)
         ring = range(4)
         rows = {
             TOKENS_AT: [1 - core],
@@ -425,10 +422,10 @@
             SECOND_AT: [2 * final_side(to) for to in ring] * 2,
             Y_FIRST_AT: [through_side(y, to) for to in ring],
             Y_SECOND_AT: [final_side(to) for to in ring],
-            Y_SLOT_AT: [2 * moved(y, to) + final_side(to) for to in ring],
+            Y_SLOT_AT: [y ^ to for to in ring],
             X_MOVED_AT: [moved(x, to) for to in ring],
             X_SECOND_AT: [final_side(to) for to in ring],
-            LEFT_AT: [order.index(to) for to in ring],
+            LEFT_AT: [x ^ to for to in ring],
             IN_AT: [4 * core],
             X_LOW_AT: [x_low],
             Y_LOW_AT: [y % 2],
@@ -440,14 +437,14 @@
 
 def on_device(tokens, grads, weight_grad):
     x_low = lax.axis_index("row_0")
-    y = lax.axis_index("row_1")
     x_high = lax.axis_index("col_0")
     core = lax.axis_index("col_1")
     index = lax.dynamic_index_in_dim(jnp.asarray(index_table()), lax.axis_index(ALL), 0, keepdims=False)
 
-    half, trace = tokens_share(index, tokens)
+    half, trace_in = share(index, tokens, D // 2, TOKENS_AT, 1, 1)
     got_in = swap(half, 1, 1)
-    one, two, trace = grads_share(index, grads, trace)
+    one, two, trace_out = share(index, grads, 1536, GRADS_AT, 8, 2)
+    trace = jnp.concatenate([trace_in, trace_out], axis=0)
     got_trace = swap(trace, 1, 1)
     got_one = swap(one, 1, 1)
     got_two = swap(two, 1, 1)
@@ -462,20 +459,20 @@
     both = keep + got
     got = second(pick(both, x, 1), X_BITS)
     both = pick(both, x, 0) + got
-    got = first(both[2:], Y_BITS)
-    both = both[:2] + got
-    got = second(pick(both, y, 1), Y_BITS)
-    both = pick(both, y, 0) + got
-    got = first(both, Z_BITS)
-    both = both + got
-    got = second(both, Z_BITS)
+    got = []
+    for mask in range(1, 4):
+        got.append(swap(both[mask], Y_BITS[mask], Y_BITS[mask]))
+    both = (both[0] + got[1]) + (got[0] + got[2])
+    got = []
+    for mask in range(1, 4):
+        got.append(swap(both, Z_BITS[mask], Z_BITS[mask]))
     own, trace = inverse(
-        inverse_in_kernel, index, [both, got], [((BLOCK, BLOCK), jnp.bfloat16), ((8, LANES), jnp.float32)]
+        inverse_in_kernel, index, [both] + got, [((BLOCK, BLOCK), jnp.bfloat16), ((8, LANES), jnp.float32)]
     )
-    got = first(own, X_BITS)
-    slots = jnp.stack([own, got])
-    got = second(slots, X_BITS)
-    slots = jnp.concatenate([slots, got], axis=0)
+    slots = [own]
+    for mask in range(1, 4):
+        slots.append(swap(own, X_BITS[mask], X_BITS[mask]))
+    slots = jnp.stack(slots)
     got = swap(slots, 1, 1)
     slots = jnp.where(core == x_low, slots, got)
     left, sums = left_product(index, slots, weight_grad)
@@ -483,7 +480,8 @@
     parts = []
     for last, got in enumerate((got_one, got_two)):
         blocks = out_blocks(index, last, grads, got)
-        blocks = trade((blocks * OUT_SCALE).astype(jnp.float16), cubes(False))
+        blocks = (blocks * OUT_SCALE).astype(jnp.float16)
+        blocks = trade(blocks, cubes(False))
         parts.append(jnp.sum(blocks.astype(jnp.float32), axis=0) * (1.0 / OUT_SCALE))
     cube = jnp.concatenate(parts, axis=0)
     cube = trade(cube, cubes(True))

time: 181 us -> 177 us (0.978)
  starting transfers between devices: 44.7 us -> 37.9 us
  Pallas kernels: 51.1 us -> 46.6 us
  waiting for transfers between devices: 47.8 us -> 52 us
  local copies, waits for them, and re-layouts: 6.66 us -> 8.89 us
    pallas_call x4, Pallas kernels: 33.1 us -> 27.7 us  [the longest x2 14.7 us: out_blocks(): pl.pallas_call(functools.partial(out_kernel, OWN_AT + 8 * last), grid_spe...]
    all_to_all x3, starting transfers between devices: 21.9 us -> 16.6 us  [trade(): lax.all_to_all(array, ALL, split_axis=0, concat_axis=0, tiled=True, axis_...]
    all_to_all x3, waiting for transfers between devices: 7.38 us -> 10.6 us  [trade(): lax.all_to_all(array, ALL, split_axis=0, concat_axis=0, tiled=True, axis_...]
    all_to_all x1, starting transfers between devices: 5.76 us -> 3.55 us  [on_device(): inverses = lax.all_to_all(own, ROW, split_axis=0, concat_axis=0, tiled=True)]
    ppermute x13 -> x16, waiting for transfers between devices: 37.2 us -> 38.2 us  [swap(): lax.ppermute(array, ALL, [(i, i ^ (far if i % 2 else near)) for i in rang...]
    ppermute x13 -> x16, starting transfers between devices: 17 us -> 17.8 us  [swap(): lax.ppermute(array, ALL, [(i, i ^ (far if i % 2 else near)) for i in rang...]
  transfers between devices with their start and end apart: 17 -> 20, of which waited for: 11 -> 11; matrix products, arithmetic and copies ran while one was open for 6% -> 7% of each run, Pallas kernels for 21% -> 17%
where the time goes in v2:
time: 177 us; the launch traced here: 176 us
  waiting for transfers between devices  52 us (29%)
  Pallas kernels  46.6 us (26%)
  starting transfers between devices  37.9 us (21%)
  blocking collectives  19.4 us (11%)
  other arithmetic  11.2 us (6%)
  local copies, waits for them, and re-layouts  8.89 us (5%)
    ppermute x16, waiting for transfers between devices, swap(): lax.ppermute(array, ALL, [(i, i ^ (far if i % 2 else near)) for i in rang...  38.2 us
    all_to_all x1, blocking collectives, on_device(): totals = lax.all_to_all(total, ALL, split_axis=0, concat_axis=0, tiled=True)  19.4 us
    ppermute x16, starting transfers between devices, swap(): lax.ppermute(array, ALL, [(i, i ^ (far if i % 2 else near)) for i in rang...  17.8 us
    all_to_all x3, starting transfers between devices, trade(): lax.all_to_all(array, ALL, split_axis=0, concat_axis=0, tiled=True, axis_...  16.6 us
    pallas_call x2, Pallas kernels, out_blocks(): pl.pallas_call(functools.partial(out_kernel, OWN_AT + 8 * last), grid_spe...  14.7 us
    pallas_call x2, Pallas kernels, share(): pl.pallas_call(functools.partial(share_kernel, chunk, first, count), in_s...  13 us
    all_to_all x3, waiting for transfers between devices, trade(): lax.all_to_all(array, ALL, split_axis=0, concat_axis=0, tiled=True, axis_...  10.6 us
    pallas_call x2, Pallas kernels, inverse(): pl.pallas_call(kernel, in_specs=[pl.BlockSpec(memory_space=pltpu.SMEM)] +...  9.04 us
  transfers between devices with their start and end apart: 20, of which 11 were waited for; matrix products, arithmetic and copies ran while one was open for 7% of the time, Pallas kernels for 17%

profile of v2, /device:TPU:1, one launch (start us, length us, event | category | flops | bytes accessed | tf_op | source)
XLA Modules:
  0.0 176.2 jit_solution(347581924652529803)
XLA Ops:
  1.2 9.1 %shard_map.47 = (bf16[256,6144]{1,0:T(8,128)(2,1)}, bf16[256,6144]{1,0:T(8,128)(2,1)}, f32[4,128]{1,0:T(4,128)}) custom-call(s32[128]{0:T(128)} %fusion.2.index, bf16[256,24576]{1,0:T(8,128)(2,1)} %own.5), custom_call_target="tpu_custom_call" | custom-call | flops 2000000000 | bytes 20000000 | tf_op jit(solution)/shard_map/pallas_call | solution.py:204
  11.8 3.9 %shard_map.46 = (bf16[256,3072]{1,0:T(8,128)(2,1)}, f32[4,128]{1,0:T(4,128)}) custom-call(s32[128]{0:T(128)} %fusion.2.index, bf16[256,6144]{1,0:T(8,128)(2,1)} %own.3), custom_call_target="tpu_custom_call" | custom-call | flops 2000000000 | bytes 20000000 | tf_op jit(solution)/shard_map/pallas_call | solution.py:204
  17.1 7.1 %collective-permute-done.1.trace_got = f32[8,128]{1,0:T(8,128)S(1)} collective-permute-done((f32[8,128]{1,0:T(8,128)S(1)}, f32[8,128]{1,0:T(8,128)S(1)}, u32[]{:S(2)}, u32[]{:S(2)}) %collective-permute-start.1) | collective-permute-done | bytes 4128 | tf_op jit(solution)/shard_map/ppermute | solution.py:39
  26.1 4.5 %cov_in.1 = (f32[2,4,200,128]{3,2,1,0:T(8,128)}, f32[2,4,200,128]{3,2,1,0:T(8,128)S(1)}) custom-call(s32[128]{0:T(128)S(1)} %copy-done, bf16[256,6144]{1,0:T(8,128)(2,1)S(1)} %copy-done.2, bf16[256,3072]{1,0:T(8,128)(2,1)S(1)} %collective-permute-done.got, f32[8,128]{1,0:T(8,128)S(1)} %pad_maximum_fusion.2.trace_own, ...), custom_call_target="tpu_custom_call" | custom-call | flops 5000000000 | bytes 5000000 | tf_op jit(solution)/shard_map/cov_in/pallas_call | solution.py:139
  33.1 10.0 %collective-permute-done.2 = f32[2,4,200,128]{3,2,1,0:T(8,128)S(1)} collective-permute-done((f32[2,4,200,128]{3,2,1,0:T(8,128)}, f32[2,4,200,128]{3,2,1,0:T(8,128)S(1)}, u32[]{:S(2)}, u32[]{:S(2)}) %collective-permute-start.2) | collective-permute-done | bytes 819232 | tf_op jit(solution)/shard_map/ppermute | solution.py:39
  43.8 7.4 %cov_out.3 = f32[8,4,192,128]{3,2,1,0:T(8,128)} custom-call(s32[128]{0:T(128)} %fusion.2.index, bf16[256,24576]{1,0:T(8,128)(2,1)} %own.5, bf16[256,6144]{1,0:T(8,128)(2,1)} %collective-permute-done.15.got), custom_call_target="tpu_custom_call" | custom-call | flops 10000000000 | bytes 10000000 | tf_op jit(solution)/shard_map/cov_out/pallas_call | solution.py:97
  51.1 3.5 %multiply_convert_fusion = f16[8,4,192,128]{3,2,1,0:T(8,128)(2,1)} fusion(f32[8,4,192,128]{3,2,1,0:T(8,128)} %cov_out.3), kind=kLoop, calls=%fused_computation.1 | loop fusion | flops 1572864 | bytes 4718592 | tf_op jit(solution)/shard_map/convert_element_type | solution.py:483
  54.6 9.4 %all-to-all-start.1 = ((f16[8,4,192,128]{3,2,1,0:T(8,128)(2,1)}), f16[8,4,192,128]{3,2,1,0:T(8,128)(2,1)S(1)}, u32[]{:S(2)}, u32[]{:S(2)}) async-start(f16[8,4,192,128]{3,2,1,0:T(8,128)(2,1)} %multiply_convert_fusion), calls=%async_computation.1 | async-start | bytes 3145728 | tf_op jit(solution)/shard_map/all_to_all | solution.py:377
  64.9 7.3 %cov_out.2 = f32[8,4,192,128]{3,2,1,0:T(8,128)} custom-call(s32[128]{0:T(128)} %fusion.2.index, bf16[256,24576]{1,0:T(8,128)(2,1)} %own.5, bf16[256,6144]{1,0:T(8,128)(2,1)} %collective-permute-done.14.got), custom_call_target="tpu_custom_call" | custom-call | flops 10000000000 | bytes 10000000 | tf_op jit(solution)/shard_map/cov_out/pallas_call | solution.py:97
  72.2 3.5 %multiply_convert_fusion.1 = f16[8,4,192,128]{3,2,1,0:T(8,128)(2,1)} fusion(f32[8,4,192,128]{3,2,1,0:T(8,128)} %cov_out.2), kind=kLoop, calls=%fused_computation.3 | loop fusion | flops 1572864 | bytes 4718592 | tf_op jit(solution)/shard_map/convert_element_type | solution.py:483
  75.7 4.9 %all-to-all-done.1 = f16[8,4,192,128]{3,2,1,0:T(8,128)(2,1)S(1)} async-done(((f16[8,4,192,128]{3,2,1,0:T(8,128)(2,1)}), f16[8,4,192,128]{3,2,1,0:T(8,128)(2,1)S(1)}, u32[]{:S(2)}, u32[]{:S(2)}) %all-to-all-start.1) | async-done | bytes 1572896 | tf_op jit(solution)/shard_map/all_to_all | solution.py:377
  80.6 3.6 %all-to-all-start = ((f16[8,4,192,128]{3,2,1,0:T(8,128)(2,1)}), f16[8,4,192,128]{3,2,1,0:T(8,128)(2,1)S(1)}, u32[]{:S(2)}, u32[]{:S(2)}) async-start(f16[8,4,192,128]{3,2,1,0:T(8,128)(2,1)} %multiply_convert_fusion.1), calls=%async_computation | async-start | bytes 3145728 | tf_op jit(solution)/shard_map/all_to_all | solution.py:377
  88.5 5.2 %collective-permute-done.4 = f32[200,128]{1,0:T(8,128)S(1)} collective-permute-done((f32[200,128]{1,0:T(8,128)S(1)}, f32[200,128]{1,0:T(8,128)S(1)}, u32[]{:S(2)}, u32[]{:S(2)}) %collective-permute-start.4) | collective-permute-done | bytes 102432 | tf_op jit(solution)/shard_map/ppermute | solution.py:39
  93.7 3.2 %collective-permute-done.5 = f32[200,128]{1,0:T(8,128)S(1)} collective-permute-done((f32[200,128]{1,0:T(8,128)S(1)}, f32[200,128]{1,0:T(8,128)S(1)}, u32[]{:S(2)}, u32[]{:S(2)}) %collective-permute-start.5) | collective-permute-done | bytes 102432 | tf_op jit(solution)/shard_map/ppermute | solution.py:39
  96.9 3.8 %collective-permute-done.6 = f32[200,128]{1,0:T(8,128)S(1)} collective-permute-done((f32[200,128]{1,0:T(8,128)S(1)}, f32[200,128]{1,0:T(8,128)S(1)}, u32[]{:S(2)}, u32[]{:S(2)}) %collective-permute-start.6) | collective-permute-done | bytes 102432 | tf_op jit(solution)/shard_map/ppermute | solution.py:39
  101.7 3.6 %collective-permute-start.8 = (f32[200,128]{1,0:T(8,128)S(1)}, f32[200,128]{1,0:T(8,128)S(1)}, u32[]{:S(2)}, u32[]{:S(2)}) collective-permute-start(f32[200,128]{1,0:T(8,128)S(1)} %fusion.1.one), channel_id=1, source_target_pairs={{0,64},{1,65},{2,66},{3,67},{4,68},{5,69},{6,70},{7,71},{8,72},{9,... | collective-permute-start | bytes 307208 | tf_op jit(solution)/shard_map/ppermute | solution.py:39
  105.6 5.1 %collective-permute-done.8.three = f32[200,128]{1,0:T(8,128)S(1)} collective-permute-done((f32[200,128]{1,0:T(8,128)S(1)}, f32[200,128]{1,0:T(8,128)S(1)}, u32[]{:S(2)}, u32[]{:S(2)}) %collective-permute-start.8) | collective-permute-done | bytes 102432 | tf_op jit(solution)/shard_map/ppermute | solution.py:39
  113.0 4.1 %shard_map.48 = (bf16[192,192]{1,0:T(8,128)(2,1)S(1)}, f32[8,128]{1,0:T(8,128)S(1)}) custom-call(s32[128]{0:T(128)S(1)} %copy-done.1, f32[200,128]{1,0:T(8,128)S(1)} %fusion.1.one, f32[200,128]{1,0:T(8,128)S(1)} %collective-permute-done.7.two, f32[200,128]{1,0:T(8,128)S(1)} %collective-permute-done.8.three, f32[200,128]{1,0:T(8,128)S(1)} %collective-permute-done.9.four), custom_call_target="tpu_custom_call" | custom-call | flops 5000000000 | bytes 200000 | tf_op jit(solution)/shard_map/pallas_call | solution.py:269
  122.6 3.5 %all-to-all-start.2 = ((f32[8,192,128]{2,1,0:T(8,128)}), f32[8,192,128]{2,1,0:T(8,128)S(1)}, u32[]{:S(2)}, u32[]{:S(2)}) async-start(f32[8,192,128]{2,1,0:T(8,128)} %pad_maximum_fusion), calls=%async_computation.2 | async-start | bytes 1572864 | tf_op jit(solution)/shard_map/all_to_all | solution.py:377
  129.2 5.8 %all-to-all-done.2.slots = f32[8,192,128]{2,1,0:T(8,128)S(1)} async-done(((f32[8,192,128]{2,1,0:T(8,128)}), f32[8,192,128]{2,1,0:T(8,128)S(1)}, u32[]{:S(2)}, u32[]{:S(2)}) %all-to-all-start.2) | async-done | bytes 786464 | tf_op jit(solution)/shard_map/all_to_all | solution.py:377
  134.9 5.0 %shard_map.49 = bf16[8,192,192]{2,1,0:T(8,128)(2,1)} custom-call(s32[128]{0:T(128)S(1)} %copy-done.1, f32[8,128]{1,0:T(8,128)S(1)} %get-tuple-element.23.trace, f32[8,192,128]{2,1,0:T(8,128)S(1)} %all-to-all-done.2.slots), custom_call_target="tpu_custom_call" | custom-call | flops 5000000000 | bytes 200000 | tf_op jit(solution)/shard_map/pallas_call | solution.py:269
  139.9 3.5 %all-to-all-start.3 = ((bf16[8,192,192]{2,1,0:T(8,128)(2,1)}), bf16[8,192,192]{2,1,0:T(8,128)(2,1)S(1)}, u32[]{:S(2)}, u32[]{:S(2)}) async-start(bf16[8,192,192]{2,1,0:T(8,128)(2,1)} %shard_map.49), calls=%async_computation.3 | async-start | bytes 1572864 | tf_op jit(solution)/shard_map/all_to_all | solution.py:489
  148.5 3.2 %all-to-all-done.3.inverses = bf16[8,192,192]{2,1,0:T(8,128)(2,1)S(1)} async-done(((bf16[8,192,192]{2,1,0:T(8,128)(2,1)}), bf16[8,192,192]{2,1,0:T(8,128)(2,1)S(1)}, u32[]{:S(2)}, u32[]{:S(2)}) %all-to-all-start.3) | async-done | bytes 589856 | tf_op jit(solution)/shard_map/all_to_all | solution.py:489
  152.1 19.4 %all_to_all.31 = f32[128,1,128]{2,1,0:T(1,128)S(1)} all-to-all(f32[128,1,128]{2,1,0:T(1,128)S(1)} %bitcast.28), channel_id=1, replica_groups=mesh['dp'=4,'row_0'=2,'row_1'=4,'col_0'=2,'col_1'=2] {'dp','row_0','row_..., dimensions={0} | all-to-all | bytes 131072 | tf_op jit(solution)/shard_map/all_to_all | solution.py:491
  (57 shorter events, 36.5 us)
Async XLA Ops:
  10.3 6.0 %copy-start.6 = (f32[4,128]{1,0:T(4,128)S(1)}, f32[4,128]{1,0:T(4,128)}, u32[]{:S(2)}) copy-start(f32[4,128]{1,0:T(4,128)} %get-tuple-element.18) | copy-start | bytes 6148
  10.3 13.9 %copy-start = (s32[128]{0:T(128)S(1)}, s32[128]{0:T(128)}, u32[]{:S(2)}) copy-start(s32[128]{0:T(128)} %fusion.2.index) | copy-start | bytes 1540
  10.3 33.4 %collective-permute-start.15 = (bf16[256,6144]{1,0:T(8,128)(2,1)}, bf16[256,6144]{1,0:T(8,128)(2,1)}, u32[]{:S(2)}, u32[]{:S(2)}) collective-permute-start(bf16[256,6144]{1,0:T(8,128)(2,1)} %get-tuple-element.25), channel_id=1, source_target_pairs={{0,1},{1,0},{2,3},{3,2},{4,5},{5,4},{6,7},{7,6},{8,9},{9,8},{10,11... | collective-permute-start | bytes 9437192 | tf_op jit(solution)/shard_map/ppermute | solution.py:39
  15.7 8.5 %collective-permute-start = (bf16[256,3072]{1,0:T(8,128)(2,1)}, bf16[256,3072]{1,0:T(8,128)(2,1)S(1)}, u32[]{:S(2)}, u32[]{:S(2)}) collective-permute-start(bf16[256,3072]{1,0:T(8,128)(2,1)} %get-tuple-element.16), channel_id=1, source_target_pairs={{0,1},{1,0},{2,3},{3,2},{4,5},{5,4},{6,7},{7,6},{8,9},{9,8},{10,11... | collective-permute-start | bytes 4718600 | tf_op jit(solution)/shard_map/ppermute | solution.py:39
  15.8 49.1 %collective-permute-start.14 = (bf16[256,6144]{1,0:T(8,128)(2,1)}, bf16[256,6144]{1,0:T(8,128)(2,1)}, u32[]{:S(2)}, u32[]{:S(2)}) collective-permute-start(bf16[256,6144]{1,0:T(8,128)(2,1)} %get-tuple-element.24), channel_id=1, source_target_pairs={{0,1},{1,0},{2,3},{3,2},{4,5},{5,4},{6,7},{7,6},{8,9},{9,8},{10,11... | collective-permute-start | bytes 9437192 | tf_op jit(solution)/shard_map/ppermute | solution.py:39
  17.0 7.2 %collective-permute-start.1 = (f32[8,128]{1,0:T(8,128)S(1)}, f32[8,128]{1,0:T(8,128)S(1)}, u32[]{:S(2)}, u32[]{:S(2)}) collective-permute-start(f32[8,128]{1,0:T(8,128)S(1)} %pad_maximum_fusion.2.trace_own), channel_id=1, source_target_pairs={{0,1},{1,0},{2,3},{3,2},{4,5},{5,4},{6,7},{7,6},{8,9},{9,8},{10,11... | collective-permute-start | bytes 12296 | tf_op jit(solution)/shard_map/ppermute | solution.py:39
  24.2 1.9 %copy-start.2 = (bf16[256,6144]{1,0:T(8,128)(2,1)S(1)}, bf16[256,6144]{1,0:T(8,128)(2,1)}, u32[]{:S(2)}) copy-start(bf16[256,6144]{1,0:T(8,128)(2,1)} %own.3) | copy-start | bytes 9437188
  30.5 12.6 %collective-permute-start.2 = (f32[2,4,200,128]{3,2,1,0:T(8,128)}, f32[2,4,200,128]{3,2,1,0:T(8,128)S(1)}, u32[]{:S(2)}, u32[]{:S(2)}) collective-permute-start(f32[2,4,200,128]{3,2,1,0:T(8,128)} %get-tuple-element.20), channel_id=1, source_target_pairs={{0,16},{1,19},{2,18},{3,17},{4,20},{5,23},{6,22},{7,21},{8,24},{9,... | collective-permute-start | bytes 2457608 | tf_op jit(solution)/shard_map/ppermute | solution.py:39
  43.3 20.7 %collective-permute-start.3 = (f32[4,200,128]{2,1,0:T(8,128)S(1)}, f32[4,200,128]{2,1,0:T(8,128)S(1)}, u32[]{:S(2)}, u32[]{:S(2)}) collective-permute-start(f32[4,200,128]{2,1,0:T(8,128)S(1)} %dynamic-slice_bitcast_fusion), channel_id=1, source_target_pairs={{0,18},{1,17},{2,16},{3,19},{4,22},{5,21},{6,20},{7,23},{8,26},{9,... | collective-permute-start | bytes 1228808 | tf_op jit(solution)/shard_map/ppermute | solution.py:39
  54.6 25.9 %all-to-all-start.1 = ((f16[8,4,192,128]{3,2,1,0:T(8,128)(2,1)}), f16[8,4,192,128]{3,2,1,0:T(8,128)(2,1)S(1)}, u32[]{:S(2)}, u32[]{:S(2)}) async-start(f16[8,4,192,128]{3,2,1,0:T(8,128)(2,1)} %multiply_convert_fusion), calls=%async_computation.1 | async-start | bytes 3145728 | tf_op jit(solution)/shard_map/all_to_all | solution.py:377
  75.7 37.4 %copy-start.1 = (s32[128]{0:T(128)S(1)}, s32[128]{0:T(128)}, u32[]{:S(2)}) copy-start(s32[128]{0:T(128)} %fusion.2.index) | copy-start | bytes 1540
  80.6 40.8 %all-to-all-start = ((f16[8,4,192,128]{3,2,1,0:T(8,128)(2,1)}), f16[8,4,192,128]{3,2,1,0:T(8,128)(2,1)S(1)}, u32[]{:S(2)}, u32[]{:S(2)}) async-start(f16[8,4,192,128]{3,2,1,0:T(8,128)(2,1)} %multiply_convert_fusion.1), calls=%async_computation | async-start | bytes 3145728 | tf_op jit(solution)/shard_map/all_to_all | solution.py:377
  85.2 8.5 %collective-permute-start.4 = (f32[200,128]{1,0:T(8,128)S(1)}, f32[200,128]{1,0:T(8,128)S(1)}, u32[]{:S(2)}, u32[]{:S(2)}) collective-permute-start(f32[200,128]{1,0:T(8,128)S(1)} %get-tuple-element.29), channel_id=1, source_target_pairs={{0,8},{1,9},{2,10},{3,11},{4,12},{5,13},{6,14},{7,15},{8,0},{9,1},... | collective-permute-start | bytes 307208 | tf_op jit(solution)/shard_map/ppermute | solution.py:39
  86.8 10.1 %collective-permute-start.5 = (f32[200,128]{1,0:T(8,128)S(1)}, f32[200,128]{1,0:T(8,128)S(1)}, u32[]{:S(2)}, u32[]{:S(2)}) collective-permute-start(f32[200,128]{1,0:T(8,128)S(1)} %get-tuple-element.28), channel_id=1, source_target_pairs={{0,4},{1,5},{2,6},{3,7},{4,0},{5,1},{6,2},{7,3},{8,12},{9,13},{10,... | collective-permute-start | bytes 307208 | tf_op jit(solution)/shard_map/ppermute | solution.py:39
  88.4 12.3 %collective-permute-start.6 = (f32[200,128]{1,0:T(8,128)S(1)}, f32[200,128]{1,0:T(8,128)S(1)}, u32[]{:S(2)}, u32[]{:S(2)}) collective-permute-start(f32[200,128]{1,0:T(8,128)S(1)} %get-tuple-element.27), channel_id=1, source_target_pairs={{0,12},{1,13},{2,14},{3,15},{4,8},{5,9},{6,10},{7,11},{8,4},{9,5},... | collective-permute-start | bytes 307208 | tf_op jit(solution)/shard_map/ppermute | solution.py:39
  101.6 3.9 %collective-permute-start.7 = (f32[200,128]{1,0:T(8,128)S(1)}, f32[200,128]{1,0:T(8,128)S(1)}, u32[]{:S(2)}, u32[]{:S(2)}) collective-permute-start(f32[200,128]{1,0:T(8,128)S(1)} %fusion.1.one), channel_id=1, source_target_pairs={{0,32},{1,33},{2,34},{3,35},{4,36},{5,37},{6,38},{7,39},{8,40},{9,... | collective-permute-start | bytes 307208 | tf_op jit(solution)/shard_map/ppermute | solution.py:39
  101.7 9.0 %collective-permute-start.8 = (f32[200,128]{1,0:T(8,128)S(1)}, f32[200,128]{1,0:T(8,128)S(1)}, u32[]{:S(2)}, u32[]{:S(2)}) collective-permute-start(f32[200,128]{1,0:T(8,128)S(1)} %fusion.1.one), channel_id=1, source_target_pairs={{0,64},{1,65},{2,66},{3,67},{4,68},{5,69},{6,70},{7,71},{8,72},{9,... | collective-permute-start | bytes 307208 | tf_op jit(solution)/shard_map/ppermute | solution.py:39
  105.3 7.7 %collective-permute-start.9 = (f32[200,128]{1,0:T(8,128)S(1)}, f32[200,128]{1,0:T(8,128)S(1)}, u32[]{:S(2)}, u32[]{:S(2)}) collective-permute-start(f32[200,128]{1,0:T(8,128)S(1)} %fusion.1.one), channel_id=1, source_target_pairs={{0,96},{1,97},{2,98},{3,99},{4,100},{5,101},{6,102},{7,103},{8,104... | collective-permute-start | bytes 307208 | tf_op jit(solution)/shard_map/ppermute | solution.py:39
  117.1 9.1 %collective-permute-start.12 = (bf16[192,192]{1,0:T(8,128)(2,1)S(1)}, bf16[192,192]{1,0:T(8,128)(2,1)S(1)}, u32[]{:S(2)}, u32[]{:S(2)}) collective-permute-start(bf16[192,192]{1,0:T(8,128)(2,1)S(1)} %get-tuple-element.21), channel_id=1, source_target_pairs={{0,18},{1,19},{2,16},{3,17},{4,22},{5,23},{6,20},{7,21},{8,26},{9,... | collective-permute-start | bytes 221192 | tf_op jit(solution)/shard_map/ppermute | solution.py:39
  118.3 7.9 %collective-permute-start.10 = (bf16[192,192]{1,0:T(8,128)(2,1)S(1)}, bf16[192,192]{1,0:T(8,128)(2,1)S(1)}, u32[]{:S(2)}, u32[]{:S(2)}) collective-permute-start(bf16[192,192]{1,0:T(8,128)(2,1)S(1)} %get-tuple-element.21), channel_id=1, source_target_pairs={{0,16},{1,17},{2,18},{3,19},{4,20},{5,21},{6,22},{7,23},{8,24},{9,... | collective-permute-start | bytes 221192 | tf_op jit(solution)/shard_map/ppermute | solution.py:39
  118.6 7.6 %collective-permute-start.11 = (bf16[192,192]{1,0:T(8,128)(2,1)S(1)}, bf16[192,192]{1,0:T(8,128)(2,1)S(1)}, u32[]{:S(2)}, u32[]{:S(2)}) collective-permute-start(bf16[192,192]{1,0:T(8,128)(2,1)S(1)} %get-tuple-element.21), channel_id=1, source_target_pairs={{0,2},{1,3},{2,0},{3,1},{4,6},{5,7},{6,4},{7,5},{8,10},{9,11},{10,... | collective-permute-start | bytes 221192 | tf_op jit(solution)/shard_map/ppermute | solution.py:39
  122.6 12.3 %all-to-all-start.2 = ((f32[8,192,128]{2,1,0:T(8,128)}), f32[8,192,128]{2,1,0:T(8,128)S(1)}, u32[]{:S(2)}, u32[]{:S(2)}) async-start(f32[8,192,128]{2,1,0:T(8,128)} %pad_maximum_fusion), calls=%async_computation.2 | async-start | bytes 1572864 | tf_op jit(solution)/shard_map/all_to_all | solution.py:377
  126.3 2.7 %collective-permute-start.13 = (bf16[4,192,192]{2,1,0:T(8,128)(2,1)S(1)}, bf16[4,192,192]{2,1,0:T(8,128)(2,1)S(1)}, u32[]{:S(2)}, u32[]{:S(2)}) collective-permute-start(bf16[4,192,192]{2,1,0:T(8,128)(2,1)S(1)} %pad_maximum_fusion.1), channel_id=1, source_target_pairs={{0,1},{1,0},{2,3},{3,2},{4,5},{5,4},{6,7},{7,6},{8,9},{9,8},{10,11... | collective-permute-start | bytes 884744 | tf_op jit(solution)/shard_map/ppermute | solution.py:39
  139.9 11.8 %all-to-all-start.3 = ((bf16[8,192,192]{2,1,0:T(8,128)(2,1)}), bf16[8,192,192]{2,1,0:T(8,128)(2,1)S(1)}, u32[]{:S(2)}, u32[]{:S(2)}) async-start(bf16[8,192,192]{2,1,0:T(8,128)(2,1)} %shard_map.49), calls=%async_computation.3 | async-start | bytes 1572864 | tf_op jit(solution)/shard_map/all_to_all | solution.py:489
  (3 other events, 4.7 us)
